TPU v7x, 256 devices: a whole 4x4x8 slice. The times are simulated.
256 devices in a mesh: row: 16 (over y, x), col: 16 (over z, core).
Axes of the slice: x: 4, y: 4, z: 8, core: 2. Of those that a mesh axis runs over, the one named last changes fastest.
Arguments:
- matrix: float32 [3, 16, 256, 3, 16, 256], P(None, 'row', None, None, 'col'), may hold values from -1.4 to 1.4, as said below
- vectors: float32 [4096, 3, 16, 256], P('col', None, 'row'), may hold values from -6 to 6
Outputs:
- reduced: float32 [3, 16, 256, 3, 16, 256], P(None, 'row', None, None, 'col')
- transformed: float32 [4096, 3, 16, 256], P('col', None, 'row')
Inputs may be any that keep to these rules, and one draw needn't show every extreme that they name: `matrix`: symmetric as the 12288 x 12288 array of its meaning.
All inputs are finite; a program needn't handle non-finite values.
Results may differ from a plain program's by a relative error of at most 0.00013.
Values sent between devices are 32-bit elements; how exact they have to be, the bound alone decides.
A program may use at most 128 MiB of HBM per device.

v0:
```python
import jax
import jax.numpy as jnp
from jax import lax
from jax.sharding import Mesh
from jax.sharding import PartitionSpec as P

COL = ("col_0", "col_1")


precise = lax.Precision.HIGHEST


def rows_for(lines, size):
    spare = -len(lines) % size
    return jnp.pad(lines, [(0, spare)] + [(0, 0)] * (lines.ndim - 1))


def laid_out(pieces, dim):
    pieces = jnp.moveaxis(pieces, 0, dim)
    shape = pieces.shape
    return pieces.reshape(*shape[:dim], shape[dim] * shape[dim + 1], *shape[dim + 2 :])


def copy_for_each(shard, axis):
    size = lax.axis_size(axis)
    return lax.all_to_all(
        jnp.broadcast_to(shard[None], (size, *shard.shape)), axis, 0, 0, tiled=True
    )


def gathered_copies(shard, axis, dim):
    return laid_out(copy_for_each(shard, axis), dim)


def split_up(shard, dim, size):
    before, after = (shard.shape[:dim], shard.shape[dim + 1 :])
    return jnp.moveaxis(shard.reshape(*before, size, -1, *after), dim, 0)


def summed_on_arrival(shard, axis, dim):
    pieces = split_up(shard, dim, lax.axis_size(axis))
    arrived = lax.all_to_all(pieces, axis, split_axis=0, concat_axis=0, tiled=True)
    return arrived.sum(axis=0)


def nested_sum(shard, axes):
    padded = rows_for(shard, lax.axis_size(axes))
    whole = gathered_copies(summed_on_arrival(padded, axes, 0), axes, 0)
    return lax.slice_in_dim(whole, 0, len(shard)).reshape(shard.shape)


def together(arrays, axis):
    line, at, outs = (jnp.concatenate([a.reshape(-1) for a in arrays]), 0, [])
    subtotal = nested_sum(line, axis)
    for a in arrays:
        outs.append(subtotal[at : at + a.size].reshape(a.shape))
        at += a.size
    return tuple(outs)


def picked_2(shard, axis, root):
    return lax.dynamic_index_in_dim(lax.all_gather(shard, axis), root, 0, keepdims=False)


def gather_axes(shard, axes, dim):
    far, near = axes
    initial = copy_for_each(shard, far)
    pieces = jnp.swapaxes(copy_for_each(initial, near), 0, 1)
    return laid_out(pieces.reshape(-1, *shard.shape), dim)


def summed_rows(shard, axes, dim):
    far, near = axes
    own = summed_on_arrival(split_up(shard, dim, lax.axis_size(far)), near, dim + 1)
    return jnp.sum(lax.all_to_all(own, far, 0, 0, tiled=True), axis=0)


def total_of(shard, axes):
    lines = shard.reshape(-1, shard.shape[-1])
    padded = rows_for(lines, lax.axis_size(axes[0]) * lax.axis_size(axes[1]))
    whole = gather_axes(summed_rows(padded, axes, 0), axes, 0)
    return lax.slice_in_dim(whole, 0, len(lines)).reshape(shard.shape)


def total_of_2(shard, axes):
    lines = shard.reshape(-1, shard.shape[-1])
    padded = rows_for(lines, lax.axis_size(axes))
    whole = gathered_copies(summed_on_arrival(padded, axes, 0), axes, 0)
    return lax.slice_in_dim(whole, 0, len(lines)).reshape(shard.shape)


def matmul(left_side, right_side):
    return jnp.dot(left_side, right_side, precision=precise, preferred_element_type=jnp.float32)


def matmul_tn(left_side, right_side):
    return lax.dot_general(
        left_side,
        right_side,
        (((0,), (0,)), ((), ())),
        precision=precise,
        preferred_element_type=jnp.float32,
    )


def matmul_nt(left_side, right_side):
    return lax.dot_general(
        left_side,
        right_side,
        (((1,), (1,)), ((), ())),
        precision=precise,
        preferred_element_type=jnp.float32,
    )


def invert_general(square):
    normal_matrix = matmul_tn(square, square)
    factor = jnp.linalg.cholesky(normal_matrix)
    return jax.scipy.linalg.cho_solve((factor, True), square.T)


def column_blocks(row_parts, my_col, rows_dev, local_cols):
    stride_count = row_parts.shape[0] // local_cols
    grouped = row_parts.reshape(local_cols, stride_count, row_parts.shape[1], row_parts.shape[2])
    picked = lax.dynamic_index_in_dim(grouped, my_col // rows_dev, 1, keepdims=False)
    return picked.reshape(local_cols * row_parts.shape[1], row_parts.shape[2])


def on_device(matrix, vectors):
    rows_dev = lax.axis_size("row")
    cols_dev = lax.axis_size(COL)
    my_row = lax.axis_index("row")
    my_col = lax.axis_index(COL)
    local_rows, _, panel_width, local_cols, _, _ = matrix.shape
    height = local_rows * panel_width
    width_local = local_cols * panel_width
    current = matrix.reshape(height, width_local)
    vector_count = vectors.shape[0]
    projected_rows = vectors.reshape(vector_count, height)
    identity = jnp.eye(panel_width, dtype=jnp.float32)
    block_ids = jnp.arange(local_rows, dtype=jnp.int32) * rows_dev + my_row
    owner_col = 0 % cols_dev
    owner_slot = 0 // cols_dev
    blocks = current.reshape(local_rows, panel_width, local_cols, panel_width)
    panel_blocks = blocks[:, :, owner_slot, :]
    below_band = (block_ids > 0)[:, None, None]
    leading = (block_ids == 1)[:, None, None]
    panel_rows = jnp.where(below_band, panel_blocks, 0.0).reshape(height, panel_width)
    gram_part = matmul_tn(panel_rows, panel_rows)
    top_part = jnp.sum(jnp.where(leading, panel_blocks, 0.0), axis=0)
    gram_full, top_panel = together((gram_part, top_part), "row")
    lower_factor = jnp.linalg.cholesky(gram_full)
    inverse_factor = jax.scipy.linalg.solve_triangular(lower_factor, identity, lower=True)
    basis_rows = matmul_nt(panel_rows, inverse_factor)
    top_basis = matmul_nt(top_panel, inverse_factor)
    kernel = invert_general(identity + top_basis)
    reflect_local = basis_rows + jnp.where(leading, identity, 0.0).reshape(height, panel_width)
    reflect_rows, kernel = (
        picked_2(reflect_local, COL, owner_col),
        picked_2(kernel, COL, owner_col),
    )
    reflect_pick = column_blocks(
        reflect_rows.reshape(local_rows, panel_width, panel_width), my_col, rows_dev, local_cols
    )
    reflect_cols = picked_2(reflect_pick, "row", my_col % rows_dev)
    image_full = total_of(matmul(current, reflect_cols), ("col_0", "col_1"))
    inner_gram = total_of_2(matmul_tn(reflect_rows, image_full), "row")
    middle = matmul(matmul_tn(kernel, inner_gram), kernel)
    update_rows = matmul(image_full, kernel) - 0.5 * matmul(reflect_rows, middle)
    update_pick = column_blocks(
        update_rows.reshape(local_rows, panel_width, panel_width), my_col, rows_dev, local_cols
    )
    update_cols = picked_2(update_pick, "row", my_col % rows_dev)
    left_side = jnp.concatenate([update_rows, reflect_rows], axis=1)
    right_side = jnp.concatenate([reflect_cols, update_cols], axis=1)
    current = current - matmul_nt(left_side, right_side)
    product = total_of_2(matmul(projected_rows, reflect_rows), "row")
    projected_rows = projected_rows - matmul_nt(matmul(product, kernel), reflect_rows)
    return (current.reshape(matrix.shape), projected_rows.reshape(vectors.shape))


def solution(mesh):
    torus = Mesh(mesh.devices.reshape(mesh.shape["row"], 8, 2), ("row", "col_0", "col_1"))
    placed = (P(None, "row", None, None, COL, None), P(COL, None, "row", None))
    return jax.shard_map(
        on_device,
        mesh=torus,
        in_specs=placed,
        out_specs=(P(None, "row", None, None, COL, None), P(COL, None, "row", None)),
        check_vma=False,
    )
```

profile of v0, /device:TPU:6, one launch (start us, length us, event | category | flops | bytes accessed | tf_op | source)
XLA Modules:
  0.0 491.8 jit_solution(11074538541935096599)
XLA Ops:
  12.2 7.4 %all-to-all-start = ((f32[16,1,8192]{2,1,0:T(1,128)}), f32[16,1,8192]{2,1,0:T(1,128)}, u32[]{:S(2)}, u32[]{:S(2)}) async-start(f32[16,1,8192]{2,1,0:T(1,128)} %all_to_all.34), calls=%async_computation | async-start | bytes 1048576 | tf_op jit(solution)/shard_map/all_to_all | solution.py:42
  19.9 8.8 %all-to-all-done = f32[16,1,8192]{2,1,0:T(1,128)} async-done(((f32[16,1,8192]{2,1,0:T(1,128)}), f32[16,1,8192]{2,1,0:T(1,128)}, u32[]{:S(2)}, u32[]{:S(2)}) %all-to-all-start) | async-done | bytes 524320 | tf_op jit(solution)/shard_map/all_to_all | solution.py:42
  31.3 6.1 %all-to-all-start.1 = ((f32[16,1,8192]{2,1,0:T(1,128)}), f32[16,1,8192]{2,1,0:T(1,128)S(1)}, u32[]{:S(2)}, u32[]{:S(2)}) async-start(f32[16,1,8192]{2,1,0:T(1,128)} %broadcast_in_dim.89), calls=%async_computation.1 | async-start | bytes 1048576 | tf_op jit(solution)/shard_map/all_to_all | solution.py:26
  38.0 7.2 %all-to-all-done.1 = f32[16,1,8192]{2,1,0:T(1,128)S(1)} async-done(((f32[16,1,8192]{2,1,0:T(1,128)}), f32[16,1,8192]{2,1,0:T(1,128)S(1)}, u32[]{:S(2)}, u32[]{:S(2)}) %all-to-all-start.1) | async-done | bytes 524320 | tf_op jit(solution)/shard_map/all_to_all | solution.py:26
  46.8 11.7 %cholesky.130 = f32[128,128]{1,0:T(8,128)S(1)} custom-call(f32[128,128]{1,0:T(8,128)S(1)} %cholesky.194), custom_call_target="Cholesky" | custom-call | tf_op jit(solution)/shard_map/jit(cholesky)/cholesky | solution.py:152
  58.6 9.8 %custom-call.18 = f32[1,128,128]{1,2,0:T(8,128)S(1)} custom-call(f32[1,128,128]{2,1,0:T(8,128)S(1)} %get-tuple-element.67), custom_call_target="InvertDiagBlocksLowerTriangular" | custom-call | tf_op jit(solution)/shard_map/jit(cholesky)/cholesky | solution.py:152
  68.9 11.7 %cholesky.147 = f32[128,128]{1,0:T(8,128)S(1)} custom-call(f32[128,128]{1,0:T(8,128)S(1)} %convolution_subtract_fusion.6), custom_call_target="Cholesky" | custom-call | tf_op jit(solution)/shard_map/jit(cholesky)/cholesky | solution.py:152
  88.0 19.7 %custom-call.19 = f32[2,128,128]{1,2,0:T(8,128)S(1)} custom-call(f32[2,128,128]{2,1,0:T(8,128)S(1)} %get-tuple-element.26), custom_call_target="InvertDiagBlocksLowerTriangular" | custom-call | tf_op jit(solution)/shard_map/jit(_solve_triangular)/triangular_solve/custom-call.1 | solution.py:153
  110.3 77.0 %all-gather.9.cloned.1.call-done = f32[12288,256]{1,0:T(8,128)} async-done(((f32[768,256]{1,0:T(8,128)}), f32[12288,256]{1,0:T(8,128)}) %all-gather.9.cloned.1.call-update) | async-done | bytes 12582928 | tf_op jit(solution)/shard_map/all_gather | solution.py:62
  191.0 11.7 %cholesky.164 = f32[128,128]{1,0:T(8,128)S(1)} custom-call(f32[128,128]{1,0:T(8,128)S(1)} %cholesky.197), custom_call_target="Cholesky" | custom-call | tf_op jit(solution)/shard_map/jit(cholesky)/cholesky | solution.py:118
  202.8 9.8 %custom-call.20 = f32[1,128,128]{1,2,0:T(8,128)S(1)} custom-call(f32[1,128,128]{2,1,0:T(8,128)S(1)} %get-tuple-element.63), custom_call_target="InvertDiagBlocksLowerTriangular" | custom-call | tf_op jit(solution)/shard_map/jit(cholesky)/cholesky | solution.py:118
  213.1 11.7 %cholesky.181 = f32[128,128]{1,0:T(8,128)S(1)} custom-call(f32[128,128]{1,0:T(8,128)S(1)} %convolution_subtract_fusion.5), custom_call_target="Cholesky" | custom-call | tf_op jit(solution)/shard_map/jit(cholesky)/cholesky | solution.py:118
  231.2 19.8 %custom-call.15 = f32[2,128,128]{1,2,0:T(8,128)S(1)} custom-call(f32[2,128,128]{2,1,0:T(8,128)S(1)} %get-tuple-element.19), custom_call_target="InvertDiagBlocksLowerTriangular" | custom-call | tf_op jit(solution)/shard_map/jit(_cho_solve)/triangular_solve | solution.py:119
  253.7 8.7 %reduce.9 = f32[3,256,3,256]{3,2,1,0:T(4,128)} reduce(f32[3,1,256,3,1,256]{5,4,3,2,1,0:T(1,128)S(1)} %copy-done, f32[]{:T(128)} %constant.173), dimensions={1,4}, to_apply=%param.5.reduce_sub_computation | reduce | bytes 4718596 | tf_op args[0]
  264.9 18.4 %all-gather.15.cloned.1.call-done = f32[12288,256]{1,0:T(8,128)} async-done(((f32[768,256]{1,0:T(8,128)}), f32[12288,256]{1,0:T(8,128)}) %all-gather.15.cloned.1.call-update) | async-done | bytes 12582928 | tf_op jit(solution)/shard_map/all_gather | solution.py:62
  285.4 5.1 %convolution_bitcast_fusion = f32[768,256]{0,1:T(8,128)} fusion(f32[768,256]{1,0:T(8,128)S(1)} %dynamic-slice_bitcast_fusion.1, f32[768,768]{1,0:T(8,128)S(1)} %bitcast.132), kind=kOutput, calls=%fused_computation.12 | convolution fusion | flops 1811939328 | bytes 3932160 | tf_op jit(solution)/shard_map/dot_general | solution.py:93
  296.5 26.1 %all_to_all.58 = f32[8,48,256]{2,1,0:T(8,128)S(1)} all-to-all(f32[8,48,256]{2,1,0:T(8,128)S(1)} %reduce_sum.56), channel_id=1, replica_groups=mesh['row'=16,'col_0'=8,'col_1'=2] {'col_0'}, dimensions={0} | all-to-all | bytes 786432 | tf_op jit(solution)/shard_map/all_to_all | solution.py:75
  329.2 11.5 %all-to-all-done.4 = f32[8,48,256]{2,1,0:T(8,128)S(1)} async-done(((f32[8,48,256]{2,1,0:T(8,128)}), f32[8,48,256]{2,1,0:T(8,128)S(1)}, u32[]{:S(2)}, u32[]{:S(2)}) %all-to-all-start.4) | async-done | bytes 393248 | tf_op jit(solution)/shard_map/all_to_all | solution.py:26
  346.1 13.3 %all_to_all.59 = f32[16,16,256]{2,1,0:T(8,128)S(1)} all-to-all(f32[16,16,256]{2,1,0:T(8,128)S(1)} %fusion.57), channel_id=1, replica_groups=mesh['row'=16,'col_0'=8,'col_1'=2] {'row'}, dimensions={0} | all-to-all | bytes 524288 | tf_op jit(solution)/shard_map/all_to_all | solution.py:42
  360.1 5.8 %all-to-all-start.7 = ((f32[16,16,256]{2,1,0:T(8,128)}), f32[16,16,256]{2,1,0:T(8,128)S(1)}, u32[]{:S(2)}, u32[]{:S(2)}) async-start(f32[16,16,256]{2,1,0:T(8,128)} %broadcast_in_dim.97), calls=%async_computation.7 | async-start | bytes 524288 | tf_op jit(solution)/shard_map/all_to_all | solution.py:26
  384.9 13.8 %all_to_all.60 = f32[16,16,256]{2,1,0:T(8,128)S(1)} all-to-all(f32[16,16,256]{2,1,0:T(8,128)S(1)} %bitcast.149), channel_id=1, replica_groups=mesh['row'=16,'col_0'=8,'col_1'=2] {'row'}, dimensions={0} | all-to-all | bytes 524288 | tf_op jit(solution)/shard_map/all_to_all | solution.py:42
  398.7 12.5 %all_to_all.57 = f32[16,16,256]{2,1,0:T(8,128)S(1)} all-to-all(f32[16,16,256]{2,1,0:T(8,128)S(1)} %broadcast_in_dim.98), channel_id=1, replica_groups=mesh['row'=16,'col_0'=8,'col_1'=2] {'row'}, dimensions={0} | all-to-all | bytes 524288 | tf_op jit(solution)/shard_map/all_to_all | solution.py:26
  420.9 51.6 %all-gather.13.cloned.1.call-done = f32[12288,256]{1,0:T(8,128)} async-done(((f32[768,256]{1,0:T(8,128)}), f32[12288,256]{1,0:T(8,128)}) %all-gather.13.cloned.1.call-update) | async-done | bytes 12582928 | tf_op jit(solution)/shard_map/all_gather | solution.py:62
  473.7 6.8 %convolution_subtract_fusion = f32[768,768]{1,0:T(8,128)} fusion(f32[768,768]{1,0:T(8,128)S(1)} %bitcast.133, f32[768,256]{1,0:T(8,128)S(1)} %copy-done.1, f32[768,256]{1,0:T(8,128)} %fusion.6, f32[768,256]{1,0:T(8,128)S(1)} %dynamic-slice_bitcast_fusion, f32[768,256]{1,0:T(8,128)} %copy-done.2), kind=kOutput, calls=%fused_computation.5 | convolution fusion | flops 3625254912 | bytes 7864320 | tf_op jit(solution)/shard_map/dot_general | solution.py:107
  (126 shorter events, 96.5 us)
Async XLA Ops:
  12.2 16.4 %all-to-all-start = ((f32[16,1,8192]{2,1,0:T(1,128)}), f32[16,1,8192]{2,1,0:T(1,128)}, u32[]{:S(2)}, u32[]{:S(2)}) async-start(f32[16,1,8192]{2,1,0:T(1,128)} %all_to_all.34), calls=%async_computation | async-start | bytes 1048576 | tf_op jit(solution)/shard_map/all_to_all | solution.py:42
  31.3 13.9 %all-to-all-start.1 = ((f32[16,1,8192]{2,1,0:T(1,128)}), f32[16,1,8192]{2,1,0:T(1,128)S(1)}, u32[]{:S(2)}, u32[]{:S(2)}) async-start(f32[16,1,8192]{2,1,0:T(1,128)} %broadcast_in_dim.89), calls=%async_computation.1 | async-start | bytes 1048576 | tf_op jit(solution)/shard_map/all_to_all | solution.py:26
  37.4 149.9 %all-gather.9.cloned.1.call-start = ((), (), s32[]{:S(2)}) async-start(), calls=%async_computation.10 | async-start | bytes 13369344 | tf_op jit(solution)/shard_map/all_gather | solution.py:62
  110.3 173.0 %all-gather.15.cloned.1.call-start = ((), (), s32[]{:S(2)}) async-start(), calls=%async_computation.13 | async-start | bytes 13369344 | tf_op jit(solution)/shard_map/all_gather | solution.py:62
  189.7 176.3 %all-gather.11.cloned.1.call-start = ((), (), s32[]{:S(2)}) async-start(), calls=%async_computation.11 | async-start | bytes 4456448 | tf_op jit(solution)/shard_map/all_gather | solution.py:62
  191.0 62.7 %copy-start = (f32[3,1,256,3,1,256]{5,4,3,2,1,0:T(1,128)S(1)}, f32[3,1,256,3,1,256]{5,4,3,2,1,0:T(1,128)}, u32[]{:S(2)}) copy-start(f32[3,1,256,3,1,256]{5,4,3,2,1,0:T(1,128)} %param.5) | copy-start | bytes 7077892
  284.5 0.9 copy-start.2
  323.4 17.2 %all-to-all-start.4 = ((f32[8,48,256]{2,1,0:T(8,128)}), f32[8,48,256]{2,1,0:T(8,128)S(1)}, u32[]{:S(2)}, u32[]{:S(2)}) async-start(f32[8,48,256]{2,1,0:T(8,128)} %broadcast_in_dim.95), calls=%async_computation.4 | async-start | bytes 786432 | tf_op jit(solution)/shard_map/all_to_all | solution.py:26
  340.6 4.6 copy-start.3
  360.1 12.2 %all-to-all-start.7 = ((f32[16,16,256]{2,1,0:T(8,128)}), f32[16,16,256]{2,1,0:T(8,128)S(1)}, u32[]{:S(2)}, u32[]{:S(2)}) async-start(f32[16,16,256]{2,1,0:T(8,128)} %broadcast_in_dim.97), calls=%async_computation.7 | async-start | bytes 524288 | tf_op jit(solution)/shard_map/all_to_all | solution.py:26
  365.9 106.6 %all-gather.13.cloned.1.call-start = ((), (), s32[]{:S(2)}) async-start(), calls=%async_computation.12 | async-start | bytes 13369344 | tf_op jit(solution)/shard_map/all_gather | solution.py:62
  368.6 9.6 %copy-start.4 = (f32[256,3,1,256]{3,2,1,0:T(1,128)S(1)}, f32[256,3,1,256]{3,2,1,0:T(1,128)}, u32[]{:S(2)}) copy-start(f32[256,3,1,256]{3,2,1,0:T(1,128)} %param.6) | copy-start | bytes 2359300
  415.4 58.3 %copy-start.1 = (f32[768,256]{1,0:T(8,128)S(1)}, f32[768,256]{1,0:T(8,128)}, u32[]{:S(2)}) copy-start(f32[768,256]{1,0:T(8,128)} %get-tuple-element.59) | copy-start | bytes 2359300
Sparse Core Ops, SparseCore 0:
  110.4 76.8 all-gather.8
  189.8 93.4 all-gather.14
  285.1 51.1 all-gather.10
  378.4 94.0 all-gather.12
where the time goes:
time: 497 us; the launch traced here: 492 us
  waiting for transfers between devices  178 us (36%)
  other arithmetic  124 us (25%)
  blocking collectives  74.6 us (15%)
  local copies, waits for them, and re-layouts  39.4 us (8%)
  matrix products  35.3 us (7%)
  starting transfers between devices  23.1 us (5%)
  between operations  17.1 us (3%)
    all_gather x4, waiting for transfers between devices, picked_2(): lax.all_gather(shard, axis)  147 us
    another operation x7, other arithmetic, on_device(): lower_factor = jnp.linalg.cholesky(gram_full)  34.7 us
    another operation x7, other arithmetic, invert_general(): factor = jnp.linalg.cholesky(normal_matrix)  34.6 us
    all_to_all x3, blocking collectives, summed_on_arrival(): lax.all_to_all(pieces, axis, split_axis=0, concat_axis=0, tiled=True)  31.5 us
    all_to_all x1, blocking collectives, summed_rows(): return jnp.sum(lax.all_to_all(own, far, 0, 0, tiled=True), axis=0)  26.1 us
    all_to_all x3, waiting for transfers between devices, copy_for_each(): lax.all_to_all(jnp.broadcast_to(shard[None], (size, *shard.shape)), axis,...  22.4 us
    another operation x3, other arithmetic, invert_general(): return jax.scipy.linalg.cho_solve((factor, True), square.T)  20.6 us
    another operation x3, other arithmetic, on_device(): jax.scipy.linalg.solve_triangular(lower_factor, identity, lower=True)  20.1 us
  transfers between devices with their start and end apart: 8, of which 7 were waited for; matrix products, arithmetic and copies ran while one was open for 22% of the time, Pallas kernels for 0%

commit v1 on v0

v1 whole, which is shorter than its diff:
```python
import functools

import jax
import jax.numpy as jnp
from jax import lax
from jax.experimental import pallas as pl
from jax.experimental.pallas import tpu as pltpu
from jax.sharding import PartitionSpec as P

MESH = pl.DeviceIdType.MESH
F32 = jnp.float32
HIGH = lax.Precision.HIGH
HIGHEST = lax.Precision.HIGHEST
STEP = 32
GROUP = 8
WIDE = 6


def dot(a, b, ca, cb, precision=HIGH):
    return lax.dot_general(
        a, b, (((ca,), (cb,)), ((), ())), precision=precision, preferred_element_type=F32
    )


def send(src, dst, ssem, rsem, axis, to):
    return pltpu.make_async_remote_copy(
        src_ref=src, dst_ref=dst, send_sem=ssem, recv_sem=rsem, device_id={axis: to}, device_id_type=MESH
    )


def loop(n, body):
    lax.fori_loop(0, n, lambda k, c: (body(k), c)[1], 0)


def greet(rows, cols, p, q):
    barrier = pltpu.get_barrier_semaphore()

    def hello_row(k):
        pl.semaphore_signal(barrier, inc=1, device_id={"row": lax.rem(p + 1 + k, rows)}, device_id_type=MESH)

    def hello_col(k):
        pl.semaphore_signal(barrier, inc=1, device_id={"col": lax.rem(q + 1 + k, cols)}, device_id_type=MESH)

    loop(rows - 1, hello_row)
    loop(cols - 1, hello_col)
    return lambda: pl.semaphore_wait(barrier, rows + cols - 2)


class Fan:
    def __init__(self, axis, size, me, ssem, rsem, src, dst, recv=None):
        self.axis, self.size, self.me = axis, size, me
        self.ssem, self.rsem, self.src, self.dst = ssem, rsem, src, dst
        self.recv = recv

    def copy(self, k):
        to = lax.rem(self.me + 1 + k, self.size)
        return send(self.src(to), self.dst(self.me), self.ssem.at[k], self.rsem.at[self.me], self.axis, to)

    def start(self):
        loop(self.size - 1, lambda k: self.copy(k).start())

    def wait_recv(self):
        def one(k):
            at = lax.rem(self.me + 1 + k, self.size)
            ref = self.dst(at)
            send(ref, ref, self.ssem.at[k], self.rsem.at[at], self.axis, at).wait_recv()

        loop(self.size - 1, one)

    def wait_send(self):
        loop(self.size - 1, lambda k: self.copy(k).wait_send())


class Scatter:
    def __init__(self, axis, size, me, root, ssem, rsem, src, dst):
        self.axis, self.size, self.me, self.root = axis, size, me, root
        self.ssem, self.rsem, self.src, self.dst = ssem, rsem, src, dst

    def copy(self, k):
        to = lax.rem(self.me + 1 + k, self.size)
        return send(self.src(to), self.dst(to), self.ssem.at[k], self.rsem, self.axis, to)

    def start(self):
        loop(self.size - 1, lambda k: self.copy(k).start())

    def wait_recv(self):
        ref = self.dst(self.me)
        send(ref, ref, self.ssem.at[0], self.rsem, self.axis, self.root).wait_recv()

    def wait_send(self):
        loop(self.size - 1, lambda k: self.copy(k).wait_send())


class Chips:
    def __init__(self, cols, q, zs, zr, ss, sr, ref):
        self.chips, self.cols, self.q, self.ref = cols // 2, cols, q, ref
        self.z, self.c = q // 2, lax.rem(q, 2)
        self.zs, self.zr, self.ss, self.sr = zs, zr, ss, sr

    def along(self, k):
        z = lax.rem(self.z + 1 + k, self.chips)
        mine = self.ref.at[self.q]
        return send(mine, mine, self.zs.at[k], self.zr.at[self.z], "col", 2 * z + self.c)

    def across(self, z):
        piece = self.ref.at[2 * z + self.c]
        return send(piece, piece, self.ss.at[z], self.sr.at[z], "col", 2 * self.z + 1 - self.c)

    def start(self):
        loop(self.chips - 1, lambda k: self.along(k).start())
        self.across(self.z).start()

    def relay(self):
        def one(k):
            z = lax.rem(self.z + 1 + k, self.chips)
            piece = self.ref.at[2 * z + self.c]
            send(piece, piece, self.zs.at[k], self.zr.at[z], "col", 2 * z + self.c).wait_recv()
            self.across(z).start()

        loop(self.chips - 1, one)

    def finish(self):
        loop(self.chips - 1, lambda k: self.along(k).wait_send())

        def one(z):
            self.across(z).wait_send()
            piece = self.ref.at[2 * z + 1 - self.c]
            send(piece, piece, self.ss.at[z], self.sr.at[z], "col", 2 * self.z + 1 - self.c).wait_recv()

        loop(self.chips, one)


def total(ref):
    size = ref.shape[0]
    acc = ref[0]
    for i in range(1, size):
        acc = acc + ref[i]
    return acc


def splat_row(x, j):
    return jnp.broadcast_to(x[j : j + 1, :], x.shape)


def small_inverse(tile, off, chol):
    row = lax.broadcasted_iota(jnp.int32, tile.shape, 0)
    lane = lax.broadcasted_iota(jnp.int32, tile.shape, 1)
    inverse = jnp.where(row == lane, 1.0, 0.0).astype(F32)
    pivots = jnp.ones_like(tile)
    for g in range(0, STEP, GROUP):
        cols = [jnp.broadcast_to(tile[:, off + g + i : off + g + i + 1], tile.shape) for i in range(GROUP)]
        for i in range(GROUP):
            j = g + i
            pivot = splat_row(cols[i], j)
            scale = 1.0 / pivot
            if chol:
                m = jnp.where(row > j, cols[i] * scale, 0.0)
                pivots = jnp.where(row == j, pivot, pivots)
            else:
                m = jnp.where(row == j, 1.0 - scale, cols[i] * scale)
            for k in range(i + 1, GROUP):
                cols[k] = cols[k] - m * splat_row(cols[k], j)
            tile = tile - m * splat_row(tile, j)
            inverse = inverse - m * splat_row(inverse, j)
    if chol:
        inverse = inverse * lax.rsqrt(pivots)
    return inverse[:, :STEP]


def eliminate(work, out, chol, halfway=None):
    size = work.shape[0]
    lane = lax.broadcasted_iota(jnp.int32, (STEP, size), 1)
    row = lax.broadcasted_iota(jnp.int32, (STEP, size), 0)
    for at in range(0, size, STEP):
        end = at + STEP
        if halfway is not None and 2 * at == size:
            halfway()
        base = at // 128 * 128
        inverse = small_inverse(work[at:end, base : base + 128], at - base, chol)
        strip = jnp.where(
            (lane >= at) & (lane < end), jnp.where(lane - at == row, 1.0, 0.0), work[at:end, :]
        )
        strip = dot(inverse, strip, 1, 0, HIGHEST)
        if chol:
            out[at:end, :] = jnp.where(lane < end, strip, 0.0)
            spans = [(end, size)]
        else:
            spans = [(0, at), (end, size)]
        for lo, hi in spans:
            if lo == hi:
                continue
            side = work[lo:hi, at:end]
            if chol:
                side = dot(side, inverse, 1, 1, HIGHEST)
            wide = lax.broadcasted_iota(jnp.int32, (hi - lo, size), 1)
            rest = jnp.where((wide >= at) & (wide < end), 0.0, work[lo:hi, :])
            work[lo:hi, :] = rest - dot(side, strip, 1, 0, HIGHEST)
        if not chol:
            work[at:end, :] = strip


def identity(size):
    row = lax.broadcasted_iota(jnp.int32, (size, size), 0)
    return jnp.where(row == lax.broadcasted_iota(jnp.int32, (size, size), 1), 1.0, 0.0).astype(F32)


def strip_of(ref, start, count, at):
    return ref[pl.ds(start * WIDE + at, count, stride=WIDE), :]


def main_kernel(
    rows, cols, alin, zlin,
    y_out, yt_out, v_out, vt_out, c_out, t_out, k_out,
    a, z, panel, panel_t, gram, landed, g_out, top_out, rows_out, cols_out, work, w,
    v, v_half, v_sum, v_land, vt, vt_land, c, c_half, c_sum, c_land, c_row, t, t_land,
    *sems,
):
    sems = iter(sems)
    p, q = lax.axis_index("row"), lax.axis_index("col")
    met = greet(rows, cols, p, q)
    first = q == 0
    chips = cols // 2
    my_z, core = q // 2, lax.rem(q, 2)
    other = 2 * my_z + 1 - core
    height, band = panel.shape
    slab, piece = rows_out.shape[1], top_out.shape[1]

    row = lax.broadcasted_iota(jnp.int32, (height, 128), 0)
    for at in range(band // 128):
        panel[:, 128 * at : 128 * (at + 1)] = jnp.where((row < band) & (p == 0), 0.0, strip_of(alin, 0, height, at))
    gram[...] = dot(panel[...], panel[...], 0, 0, HIGHEST).reshape(gram.shape)
    for at in range(WIDE):
        part = strip_of(alin, 0, band, at)
        if at < band // 128:
            part = jnp.where(q == 0, 0.0, part)
        panel_t[:, :, 128 * at : 128 * (at + 1)] = part.reshape(rows, band // rows, 128)

    def top_piece(to):
        return panel.at[pl.ds(pl.multiple_of(to * piece, piece), piece), :]

    def row_piece(to):
        return panel.at[pl.ds(pl.multiple_of(to * slab, slab), slab), :]

    def fan(axis, size, me, src, dst):
        return Fan(axis, size, me, next(sems), next(sems), src, dst)

    def cut(axis, size, me, root, src, dst):
        return Scatter(axis, size, me, root, next(sems), next(sems), src, dst)

    def ring(ref):
        return Chips(cols, q, next(sems), next(sems), next(sems), next(sems), ref)

    reduce = fan("row", rows, p, lambda to: gram.at[to], lambda at: landed.at[at])
    g_wide = fan("row", rows, p, lambda to: g_out.at[p], lambda at: g_out.at[at])
    t_wide = fan("row", rows, p, lambda to: top_out.at[p], lambda at: top_out.at[at])
    c_wide = fan("row", rows, p, lambda to: cols_out.at[p], lambda at: cols_out.at[at])
    vt_cut = fan("row", rows, p, lambda to: vt.at[to], lambda at: vt_land.at[at])
    pt_cut = fan("row", rows, p, lambda to: t.at[to], lambda at: t_land.at[at])
    pc_wide = fan("row", rows, p, lambda to: c_row.at[p], lambda at: c_row.at[at])
    vt_all = fan("row", rows, p, lambda to: vt_out.at[p], lambda at: vt_out.at[at])
    pt_all = fan("row", rows, p, lambda to: t_out.at[p], lambda at: t_out.at[at])
    g_down = cut("col", cols, q, 0, lambda to: g_out.at[p], lambda to: g_out.at[p])
    t_cut = cut("row", rows, p, 1, top_piece, lambda to: top_out.at[to])
    t_down = cut("col", cols, q, 0, lambda to: top_out.at[p], lambda to: top_out.at[p])
    r_cut = cut("col", cols, q, 0, row_piece, lambda to: rows_out.at[to])
    c_cut = cut("row", rows, p, 0, lambda to: panel_t.at[to], lambda to: cols_out.at[to])
    r_wide, v_all, c_all = ring(rows_out), ring(v_out), ring(c_out)

    met()

    @pl.when(first)
    def _():
        reduce.start()

        @pl.when(p == 1)
        def _():
            t_cut.start()

        r_cut.start()

    @pl.when(p == 0)
    def _():
        c_cut.start()

    @pl.when(first)
    def _():
        landed[p] = gram[p]
        rows_out[0] = panel[:slab, :]

        @pl.when(p == 1)
        def _():
            top_out[1] = panel[piece : 2 * piece, :]

        reduce.wait_recv()
        g_out[p] = total(landed)
        g_down.start()

    @pl.when(p == 0)
    def _():
        cols_out[0] = panel_t[0]

    @pl.when(jnp.logical_not(first))
    def _():
        g_down.wait_recv()

    g_wide.start()

    @pl.when(jnp.logical_not(first))
    def _():
        r_cut.wait_recv()

    r_wide.start()

    @pl.when(p != 0)
    def _():
        c_cut.wait_recv()

    c_wide.start()

    @pl.when(first)
    def _():
        @pl.when(p != 1)
        def _():
            t_cut.wait_recv()

        t_down.start()

    @pl.when(jnp.logical_not(first))
    def _():
        t_down.wait_recv()

    t_wide.start()
    for at in range(WIDE):
        a[:, 128 * at : 128 * (at + 1)] = strip_of(alin, 0, height, at)
        z[:, 128 * at : 128 * (at + 1)] = strip_of(zlin, 0, z.shape[0], at)
    g_wide.wait_recv()

    work[...] = g_out[...].reshape(band, band)
    eliminate(work, w, True, r_wide.relay)

    c_wide.wait_recv()
    yt_out[...] = dot(w[...], cols_out[...].reshape(band, height), 1, 0)
    r_wide.finish()
    y_out[...] = dot(rows_out[...].reshape(height, band), w[...], 1, 1)

    @pl.when(p == 1)
    def _():
        y_out[:band, :] = y_out[:band, :] + identity(band)

    @pl.when(q == 1)
    def _():
        yt_out[:, :band] = yt_out[:, :band] + identity(band)

    vt[...] = dot(y_out[...], a[...], 0, 0).reshape(vt.shape)
    vt_cut.start()

    image = dot(a[...], yt_out[...], 1, 1)
    for i in range(cols):
        v[i % 2, i // 2] = image[i * slab : (i + 1) * slab, :]
    v_swap = send(v.at[1 - core], v_half, next(sems), next(sems), "col", other)
    v_swap.start()
    t[...] = dot(z[...], y_out[...], 1, 0).reshape(t.shape)
    pt_cut.start()
    inner = dot(y_out[...], image, 0, 0)
    for i in range(cols):
        c[i % 2, i // 2] = inner[i * piece : (i + 1) * piece, :]
    c_swap = send(c.at[1 - core], c_half, next(sems), next(sems), "col", other)
    c_swap.start()
    vt_land[p] = vt[p]
    t_land[p] = t[p]

    def along(src, land):
        ss, rs = next(sems), next(sems)

        def copy(k):
            to = lax.rem(my_z + 1 + k, chips)
            return send(src.at[to], land.at[my_z], ss.at[k], rs.at[my_z], "col", 2 * to + core)

        def recv(k):
            at = lax.rem(my_z + 1 + k, chips)
            send(src.at[at], land.at[at], ss.at[k], rs.at[at], "col", 2 * at + core).wait_recv()

        return copy, recv

    v_copy, v_recv = along(v_sum, v_land)
    c_copy, c_recv = along(c_sum, c_land)
    v_swap.wait_recv()

    def v_add(i):
        v_sum[i] = v[core, i] + v_half[i]

    loop(chips, v_add)
    loop(chips - 1, lambda k: v_copy(k).start())
    c_swap.wait_recv()

    def c_add(i):
        c_sum[i] = c[core, i] + c_half[i]

    loop(chips, c_add)
    loop(chips - 1, lambda k: c_copy(k).start())
    v_land[my_z] = v_sum[my_z]
    c_land[my_z] = c_sum[my_z]

    t_wide.wait_recv()
    k_out[...] = identity(band) + dot(top_out[...].reshape(band, band), w[...], 1, 1, HIGHEST)
    eliminate(k_out, None, False)

    loop(chips - 1, c_recv)
    c_row[p] = total(c_land)
    pc_wide.start()

    vt_cut.wait_recv()
    vt_out[p] = total(vt_land)
    vt_all.start()

    loop(chips - 1, v_recv)
    v_out[q] = total(v_land)
    v_all.start()

    pt_cut.wait_recv()
    t_out[p] = total(t_land)
    pt_all.start()

    pc_wide.wait_recv()
    c_out[q] = total(c_row)
    c_all.start()

    v_all.relay()
    c_all.relay()
    vt_all.wait_recv()
    pt_all.wait_recv()
    v_all.finish()
    c_all.finish()

    @pl.when(first)
    def _():
        reduce.wait_send()

        @pl.when(p == 1)
        def _():
            t_cut.wait_send()

        r_cut.wait_send()
        g_down.wait_send()
        t_down.wait_send()

    @pl.when(p == 0)
    def _():
        c_cut.wait_send()

    v_swap.wait_send()
    c_swap.wait_send()
    loop(chips - 1, lambda k: v_copy(k).wait_send())
    loop(chips - 1, lambda k: c_copy(k).wait_send())
    for done in (g_wide, t_wide, c_wide, vt_cut, pt_cut, pc_wide, vt_all, pt_all):
        done.wait_send()


def main(rows, cols, band, alin, zlin):
    height = alin.shape[0] // WIDE
    count = zlin.shape[0] // WIDE
    chips, slab, piece, tp = cols // 2, height // cols, band // cols, count // rows
    dma = pltpu.SemaphoreType.DMA
    fan = [dma((rows,))] * 2
    cut = [dma((rows,)), dma]
    ring = [dma((chips,))] * 4
    half = [dma((chips,))] * 2
    vmem = pl.BlockSpec(memory_space=pltpu.VMEM)
    flat = (height, band)
    small = (rows, piece, band)
    outs = [flat, (band, height), (cols, slab, band), (rows, piece, height), (cols, piece, band), (rows, tp, band), (band, band)]
    scratch = [
        (height, height), (count, height), flat, (rows, piece, height), small, small, small, small,
        (cols, slab, band), (rows, piece, height), (band, band), (band, band),
        (2, chips, slab, band), (chips, slab, band), (chips, slab, band), (chips, slab, band),
        (rows, piece, height), (rows, piece, height),
        (2, chips, piece, band), (chips, piece, band), (chips, piece, band), (chips, piece, band), small,
        (rows, tp, band), (rows, tp, band),
    ]
    return pl.pallas_call(
        functools.partial(main_kernel, rows, cols),
        out_shape=tuple(jax.ShapeDtypeStruct(s, F32) for s in outs),
        in_specs=[vmem] * 2,
        out_specs=(vmem,) * len(outs),
        scratch_shapes=[pltpu.VMEM(s, F32) for s in scratch] + fan * 9 + cut * 5 + ring * 3 + [dma] * 4 + half * 2,
        compiler_params=pltpu.CompilerParams(collective_id=0, has_side_effects=True),
        name="main",
    )(alin, zlin)


def update_kernel(alin, zlin, y, yt, v, vt, c, t, k, a_out, z_out):
    height, band = y.shape
    count = zlin.shape[0] // WIDE
    image, image_t = v[...].reshape(height, band), vt[...].reshape(band, height)
    half = 0.5 * dot(dot(k[...], c[...].reshape(band, band), 0, 0), k[...], 1, 0)
    x = dot(image, k[...], 1, 0) - dot(y[...], half, 1, 0)
    xt = dot(k[...], image_t, 0, 0) - dot(half, yt[...], 0, 0)
    tk = dot(t[...].reshape(count, band), k[...], 1, 0)
    for lo in range(0, height, band):
        move = dot(x, yt[:, lo : lo + band], 1, 0) + dot(y[...], xt[:, lo : lo + band], 1, 0)
        turn = dot(tk, y[lo : lo + band, :], 1, 1)
        for i in range(band // 128):
            at = lo // 128 + i
            lanes = slice(128 * i, 128 * (i + 1))
            a_out[pl.ds(at, height, stride=WIDE), :] = strip_of(alin, 0, height, at) - move[:, lanes]
            z_out[pl.ds(at, count, stride=WIDE), :] = strip_of(zlin, 0, count, at) - turn[:, lanes]


def update(alin, zlin, *rest):
    vmem = pl.BlockSpec(memory_space=pltpu.VMEM)
    return pl.pallas_call(
        update_kernel,
        out_shape=(jax.ShapeDtypeStruct(alin.shape, F32), jax.ShapeDtypeStruct(zlin.shape, F32)),
        in_specs=[vmem] * (2 + len(rest)),
        out_specs=(vmem,) * 2,
        name="update",
    )(alin, zlin, *rest)


def on_device(rows, cols, matrix, vectors):
    band = matrix.shape[2]
    alin = matrix.reshape(-1, 128)
    zlin = vectors.reshape(-1, 128)
    a, z = update(alin, zlin, *main(rows, cols, band, alin, zlin))
    return a.reshape(matrix.shape), z.reshape(vectors.shape)


def solution(mesh):
    specs = (P(None, "row", None, None, "col", None), P("col", None, "row", None))
    return jax.shard_map(
        functools.partial(on_device, mesh.shape["row"], mesh.shape["col"]),
        mesh=mesh,
        in_specs=specs,
        out_specs=specs,
        check_vma=False,
    )
```

time: 497 us -> 101 us (0.20); the launches traced: 492 us -> 101 us
  waiting for transfers between devices: 178 us -> 0 us
  other arithmetic: 124 us -> 0 us
  Pallas kernels: 0 us -> 100 us
  blocking collectives: 74.6 us -> 0 us
  local copies, waits for them, and re-layouts: 39.4 us -> 0 us
  matrix products: 35.3 us -> 0 us
  starting transfers between devices: 23.1 us -> 0 us
  between operations: 17.1 us -> 0.64 us
    all_gather x4 -> x0, waiting for transfers between devices: 147 us -> none  [picked_2(): lax.all_gather(shard, axis)]
    another operation x20 -> x0, other arithmetic: 110 us -> none  [the longest x7 34.7 us: on_device(): lower_factor = jnp.linalg.cholesky(gram_full)]
    pallas_call x0 -> x2, Pallas kernels: none -> 100 us  [the longest x1 91.6 us: main(): pl.pallas_call(functools.partial(main_kernel, rows, cols), out_shape=tupl...]
    all_to_all x6 -> x0, blocking collectives: 74.6 us -> none  [the longest x3 31.5 us: summed_on_arrival(): lax.all_to_all(pieces, axis, split_axis=0, concat_axis=0, tiled=True)]
    dot_general x14 -> x0, matrix products: 31.6 us -> none  [the longest x6 15.4 us: matmul(): jnp.dot(left_side, right_side, precision=precise, preferred_element_type=...]
    all_to_all x4 -> x0, waiting for transfers between devices: 31.1 us -> none  [the longest x3 22.4 us: copy_for_each(): lax.all_to_all(jnp.broadcast_to(shard[None], (size, *shard.shape)), axis,...]
    all_to_all x4 -> x0, starting transfers between devices: 22.8 us -> none  [the longest x3 15.4 us: copy_for_each(): lax.all_to_all(jnp.broadcast_to(shard[None], (size, *shard.shape)), axis,...]
    unnamed x2 -> x0, other arithmetic: 11.9 us -> none
  transfers between devices with their start and end apart: 8 -> 0, of which waited for: 7 -> 0; matrix products, arithmetic and copies ran while one was open for 22% -> 0% of each run, Pallas kernels for 0% -> 0%
where the time goes in v1:
time: 101 us
  Pallas kernels  100 us (99%)
    pallas_call x1, Pallas kernels, main(): pl.pallas_call(functools.partial(main_kernel, rows, cols), out_shape=tupl...  91.6 us
    pallas_call x1, Pallas kernels, update(): pl.pallas_call(update_kernel, out_shape=(jax.ShapeDtypeStruct(alin.shape,...  8.81 us

profile of v1, /device:TPU:6, one launch (start us, length us, event | category | flops | bytes accessed | tf_op | source)
XLA Modules:
  0.0 101.0 jit_solution(2582583579265440850)
XLA Ops:
  0.6 91.6 %main.1 = (f32[768,256]{1,0:T(8,128)}, f32[256,768]{1,0:T(8,128)}, f32[16,48,256]{2,1,0:T(8,128)}, f32[16,16,768]{2,1,0:T(8,128)}, f32[16,16,256]{2,1,0:T(8,128)...) custom-call(f32[4608,128]{1,0:T(8,128)} %bitcast.4, f32[1536,128]{1,0:T(8,128)} %bitcast.6), custom_call_target="tpu_custom_call" | custom-call | tf_op jit(solution)/shard_map/main/pallas_call | solution.py:480
  92.2 8.8 %update.1 = (f32[4608,128]{1,0:T(8,128)}, f32[1536,128]{1,0:T(8,128)}) custom-call(f32[4608,128]{1,0:T(8,128)} %bitcast.5, f32[1536,128]{1,0:T(8,128)} %bitcast.7, f32[768,256]{1,0:T(8,128)} %get-tuple-element.11.y, f32[256,768]{1,0:T(8,128)} %get-tuple-element.12.yt, f32[16,48,256]{2,1,0:T(8,128)} %get-tuple-element.13.v, ...), custom_call_target="tpu_custom_call" | custom-call | tf_op jit(solution)/shard_map/update/pallas_call | solution.py:511

commit v2 on v1

--- a/solution.py
+++ b/solution.py
@@ -12,7 +12,7 @@
 HIGH = lax.Precision.HIGH
 HIGHEST = lax.Precision.HIGHEST
 STEP = 32
-GROUP = 8
+GROUP = 16
 WIDE = 6
 
 
@@ -209,13 +209,17 @@
 
 
 def main_kernel(
-    rows, cols, alin, zlin,
+    rows, cols, a_hbm, z_hbm,
     y_out, yt_out, v_out, vt_out, c_out, t_out, k_out,
-    a, z, panel, panel_t, gram, landed, g_out, top_out, rows_out, cols_out, work, w,
+    alin, zlin, a, z, panel, panel_t, gram, landed, g_out, top_out, rows_out, cols_out, work, w,
     v, v_half, v_sum, v_land, vt, vt_land, c, c_half, c_sum, c_land, c_row, t, t_land,
     *sems,
 ):
     sems = iter(sems)
+    a_in = pltpu.make_async_copy(a_hbm, alin, next(sems))
+    z_in = pltpu.make_async_copy(z_hbm, zlin, next(sems))
+    a_in.start()
+    z_in.start()
     p, q = lax.axis_index("row"), lax.axis_index("col")
     met = greet(rows, cols, p, q)
     first = q == 0
@@ -225,16 +229,11 @@
     height, band = panel.shape
     slab, piece = rows_out.shape[1], top_out.shape[1]
 
+    a_in.wait()
     row = lax.broadcasted_iota(jnp.int32, (height, 128), 0)
     for at in range(band // 128):
         panel[:, 128 * at : 128 * (at + 1)] = jnp.where((row < band) & (p == 0), 0.0, strip_of(alin, 0, height, at))
     gram[...] = dot(panel[...], panel[...], 0, 0, HIGHEST).reshape(gram.shape)
-    for at in range(WIDE):
-        part = strip_of(alin, 0, band, at)
-        if at < band // 128:
-            part = jnp.where(q == 0, 0.0, part)
-        panel_t[:, :, 128 * at : 128 * (at + 1)] = part.reshape(rows, band // rows, 128)
-
     def top_piece(to):
         return panel.at[pl.ds(pl.multiple_of(to * piece, piece), piece), :]
 
@@ -280,6 +279,11 @@
 
     @pl.when(p == 0)
     def _():
+        for at in range(WIDE):
+            part = strip_of(alin, 0, band, at)
+            if at < band // 128:
+                part = jnp.where(q == 0, 0.0, part)
+            panel_t[:, :, 128 * at : 128 * (at + 1)] = part.reshape(rows, band // rows, 128)
         c_cut.start()
 
     @pl.when(first)
@@ -330,6 +334,7 @@
         t_down.wait_recv()
 
     t_wide.start()
+    z_in.wait()
     for at in range(WIDE):
         a[:, 128 * at : 128 * (at + 1)] = strip_of(alin, 0, height, at)
         z[:, 128 * at : 128 * (at + 1)] = strip_of(zlin, 0, z.shape[0], at)
@@ -338,59 +343,59 @@
     work[...] = g_out[...].reshape(band, band)
     eliminate(work, w, True, r_wide.relay)
 
+    def along(src, land):
+        ss, rs = next(sems), next(sems)
+
+        def copy(k):
+            to = lax.rem(my_z + 1 + k, chips)
+            return send(src.at[to], land.at[my_z], ss.at[k], rs.at[my_z], "col", 2 * to + core)
+
+        def recv(k):
+            at = lax.rem(my_z + 1 + k, chips)
+            send(src.at[at], land.at[at], ss.at[k], rs.at[at], "col", 2 * at + core).wait_recv()
+
+        return copy, recv
+
     c_wide.wait_recv()
     yt_out[...] = dot(w[...], cols_out[...].reshape(band, height), 1, 0)
-    r_wide.finish()
-    y_out[...] = dot(rows_out[...].reshape(height, band), w[...], 1, 1)
-
-    @pl.when(p == 1)
-    def _():
-        y_out[:band, :] = y_out[:band, :] + identity(band)
 
     @pl.when(q == 1)
     def _():
         yt_out[:, :band] = yt_out[:, :band] + identity(band)
-
-    vt[...] = dot(y_out[...], a[...], 0, 0).reshape(vt.shape)
-    vt_cut.start()
 
     image = dot(a[...], yt_out[...], 1, 1)
     for i in range(cols):
         v[i % 2, i // 2] = image[i * slab : (i + 1) * slab, :]
     v_swap = send(v.at[1 - core], v_half, next(sems), next(sems), "col", other)
     v_swap.start()
-    t[...] = dot(z[...], y_out[...], 1, 0).reshape(t.shape)
-    pt_cut.start()
+    r_wide.finish()
+    y_out[...] = dot(rows_out[...].reshape(height, band), w[...], 1, 1)
+
+    @pl.when(p == 1)
+    def _():
+        y_out[:band, :] = y_out[:band, :] + identity(band)
+
+    vt[...] = dot(y_out[...], a[...], 0, 0).reshape(vt.shape)
+    vt_cut.start()
+    v_swap.wait_recv()
+
+    def v_add(i):
+        v_sum[i] = v[core, i] + v_half[i]
+
+    loop(chips, v_add)
+    v_copy, v_recv = along(v_sum, v_land)
+    loop(chips - 1, lambda k: v_copy(k).start())
     inner = dot(y_out[...], image, 0, 0)
     for i in range(cols):
         c[i % 2, i // 2] = inner[i * piece : (i + 1) * piece, :]
     c_swap = send(c.at[1 - core], c_half, next(sems), next(sems), "col", other)
     c_swap.start()
+    t[...] = dot(z[...], y_out[...], 1, 0).reshape(t.shape)
+    pt_cut.start()
     vt_land[p] = vt[p]
     t_land[p] = t[p]
 
-    def along(src, land):
-        ss, rs = next(sems), next(sems)
-
-        def copy(k):
-            to = lax.rem(my_z + 1 + k, chips)
-            return send(src.at[to], land.at[my_z], ss.at[k], rs.at[my_z], "col", 2 * to + core)
-
-        def recv(k):
-            at = lax.rem(my_z + 1 + k, chips)
-            send(src.at[at], land.at[at], ss.at[k], rs.at[at], "col", 2 * at + core).wait_recv()
-
-        return copy, recv
-
-    v_copy, v_recv = along(v_sum, v_land)
     c_copy, c_recv = along(c_sum, c_land)
-    v_swap.wait_recv()
-
-    def v_add(i):
-        v_sum[i] = v[core, i] + v_half[i]
-
-    loop(chips, v_add)
-    loop(chips - 1, lambda k: v_copy(k).start())
     c_swap.wait_recv()
 
     def c_add(i):
@@ -470,7 +475,7 @@
     small = (rows, piece, band)
     outs = [flat, (band, height), (cols, slab, band), (rows, piece, height), (cols, piece, band), (rows, tp, band), (band, band)]
     scratch = [
-        (height, height), (count, height), flat, (rows, piece, height), small, small, small, small,
+        alin.shape, zlin.shape, (height, height), (count, height), flat, (rows, piece, height), small, small, small, small,
         (cols, slab, band), (rows, piece, height), (band, band), (band, band),
         (2, chips, slab, band), (chips, slab, band), (chips, slab, band), (chips, slab, band),
         (rows, piece, height), (rows, piece, height),
@@ -480,10 +485,10 @@
     return pl.pallas_call(
         functools.partial(main_kernel, rows, cols),
         out_shape=tuple(jax.ShapeDtypeStruct(s, F32) for s in outs),
-        in_specs=[vmem] * 2,
+        in_specs=[pl.BlockSpec(memory_space=pltpu.HBM)] * 2,
         out_specs=(vmem,) * len(outs),
-        scratch_shapes=[pltpu.VMEM(s, F32) for s in scratch] + fan * 9 + cut * 5 + ring * 3 + [dma] * 4 + half * 2,
-        compiler_params=pltpu.CompilerParams(collective_id=0, has_side_effects=True),
+        scratch_shapes=[pltpu.VMEM(s, F32) for s in scratch] + [dma] * 2 + fan * 9 + cut * 5 + ring * 3 + [dma] * 2 + half + [dma] * 2 + half,
+        compiler_params=pltpu.CompilerParams(collective_id=0, has_side_effects=True, vmem_limit_bytes=50 * 2**20),
         name="main",
     )(alin, zlin)
 
@@ -513,6 +518,7 @@
         out_shape=(jax.ShapeDtypeStruct(alin.shape, F32), jax.ShapeDtypeStruct(zlin.shape, F32)),
         in_specs=[vmem] * (2 + len(rest)),
         out_specs=(vmem,) * 2,
+        compiler_params=pltpu.CompilerParams(vmem_limit_bytes=24 * 2**20),
         name="update",
     )(alin, zlin, *rest)
 

time: 101 us -> 90.2 us (0.89)
  Pallas kernels: 100 us -> 89.5 us
    pallas_call x1, Pallas kernels: 91.6 us -> 83.6 us  [main(): pl.pallas_call(functools.partial(main_kernel, rows, cols), out_shape=tupl...]
    pallas_call x1, Pallas kernels: 8.81 us -> 5.85 us  [update(): pl.pallas_call(update_kernel, out_shape=(jax.ShapeDtypeStruct(alin.shape,...]
where the time goes in v2:
time: 90.2 us
  Pallas kernels  89.5 us (99%)
    pallas_call x1, Pallas kernels, main(): pl.pallas_call(functools.partial(main_kernel, rows, cols), out_shape=tupl...  83.6 us
    pallas_call x1, Pallas kernels, update(): pl.pallas_call(update_kernel, out_shape=(jax.ShapeDtypeStruct(alin.shape,...  5.85 us

profile of v2, /device:TPU:6, one launch (start us, length us, event | category | flops | bytes accessed | tf_op | source)
XLA Modules:
  0.0 90.2 jit_solution(10198425510218619891)
XLA Ops:
  0.6 0.0 copy-start.1
  0.6 0.0 copy-start
  0.6 83.6 %main.1 = (f32[768,256]{1,0:T(8,128)S(1)}, f32[256,768]{1,0:T(8,128)S(1)}, f32[16,48,256]{2,1,0:T(8,128)S(1)}, f32[16,16,768]{2,1,0:T(8,128)S(1)}, f32[16,16,256...) custom-call(f32[4608,128]{1,0:T(8,128)} %bitcast.4, f32[1536,128]{1,0:T(8,128)} %bitcast.6), custom_call_target="tpu_custom_call" | custom-call | tf_op jit(solution)/shard_map/main/pallas_call | solution.py:485
  84.3 0.0 copy-done.1
  84.3 0.0 copy-done
  84.3 5.8 %update.1 = (f32[4608,128]{1,0:T(8,128)}, f32[1536,128]{1,0:T(8,128)}) custom-call(f32[4608,128]{1,0:T(8,128)S(1)} %bitcast.5, f32[1536,128]{1,0:T(8,128)S(1)} %bitcast.7, f32[768,256]{1,0:T(8,128)S(1)} %get-tuple-element.11.y, f32[256,768]{1,0:T(8,128)S(1)} %get-tuple-element.12.yt, f32[16,48,256]{2,1,0:T(8,128)S(1)} %get-tuple-element.13.v, ...), custom_call_target="tpu_custom_call" | custom-call | tf_op jit(solution)/shard_map/update/pallas_call | solution.py:516
Async XLA Ops:
  0.6 83.7 %copy-start.1 = (f32[256,3,1,256]{3,2,1,0:T(1,128)S(1)}, f32[256,3,1,256]{3,2,1,0:T(1,128)}, u32[]{:S(2)}) copy-start(f32[256,3,1,256]{3,2,1,0:T(1,128)} %param.3) | copy-start | bytes 2359300
  0.6 83.7 %copy-start = (f32[3,1,256,3,1,256]{5,4,3,2,1,0:T(1,128)S(1)}, f32[3,1,256,3,1,256]{5,4,3,2,1,0:T(1,128)}, u32[]{:S(2)}) copy-start(f32[3,1,256,3,1,256]{5,4,3,2,1,0:T(1,128)} %param.2) | copy-start | bytes 7077892

commit v3 on v2

--- a/solution.py
+++ b/solution.py
@@ -11,7 +11,7 @@
 F32 = jnp.float32
 HIGH = lax.Precision.HIGH
 HIGHEST = lax.Precision.HIGHEST
-STEP = 32
+STEP = 64
 GROUP = 16
 WIDE = 6
 
@@ -92,18 +92,18 @@
 
 
 class Chips:
-    def __init__(self, cols, q, zs, zr, ss, sr, ref):
-        self.chips, self.cols, self.q, self.ref = cols // 2, cols, q, ref
+    def __init__(self, cols, q, zs, zr, ss, sr, at):
+        self.chips, self.cols, self.q, self.at = cols // 2, cols, q, at
         self.z, self.c = q // 2, lax.rem(q, 2)
         self.zs, self.zr, self.ss, self.sr = zs, zr, ss, sr
 
     def along(self, k):
         z = lax.rem(self.z + 1 + k, self.chips)
-        mine = self.ref.at[self.q]
+        mine = self.at(self.q)
         return send(mine, mine, self.zs.at[k], self.zr.at[self.z], "col", 2 * z + self.c)
 
     def across(self, z):
-        piece = self.ref.at[2 * z + self.c]
+        piece = self.at(2 * z + self.c)
         return send(piece, piece, self.ss.at[z], self.sr.at[z], "col", 2 * self.z + 1 - self.c)
 
     def start(self):
@@ -113,7 +113,7 @@
     def relay(self):
         def one(k):
             z = lax.rem(self.z + 1 + k, self.chips)
-            piece = self.ref.at[2 * z + self.c]
+            piece = self.at(2 * z + self.c)
             send(piece, piece, self.zs.at[k], self.zr.at[z], "col", 2 * z + self.c).wait_recv()
             self.across(z).start()
 
@@ -124,7 +124,7 @@
 
         def one(z):
             self.across(z).wait_send()
-            piece = self.ref.at[2 * z + 1 - self.c]
+            piece = self.at(2 * z + 1 - self.c)
             send(piece, piece, self.ss.at[z], self.sr.at[z], "col", 2 * self.z + 1 - self.c).wait_recv()
 
         loop(self.chips, one)
@@ -142,29 +142,57 @@
     return jnp.broadcast_to(x[j : j + 1, :], x.shape)
 
 
-def small_inverse(tile, off, chol):
+def small_factor(tile, off):
     row = lax.broadcasted_iota(jnp.int32, tile.shape, 0)
     lane = lax.broadcasted_iota(jnp.int32, tile.shape, 1)
     inverse = jnp.where(row == lane, 1.0, 0.0).astype(F32)
-    pivots = jnp.ones_like(tile)
+    done, pivots = [], []
+    for g in range(0, STEP, GROUP):
+        cols = [jnp.broadcast_to(tile[:, off + g + i : off + g + i + 1], tile.shape) for i in range(GROUP)]
+        row = lax.broadcasted_iota(jnp.int32, tile.shape, 0)
+        for i in range(0, GROUP, 2):
+            here, there = cols[i], cols[i + 1]
+            a, b, d = splat_row(here, i), splat_row(there, i), splat_row(there, i + 1)
+            det = a * d - b * b
+            over_a, over_det = 1.0 / a, 1.0 / det
+            pivots += [a[:1, :], (det * over_a)[:1, :]]
+            m0 = jnp.where(row > i + 1, (here * d - there * b) * over_det, jnp.where(row == i + 1, b * over_a, 0.0))
+            m1 = jnp.where(row > i + 1, (there * a - here * b) * over_det, 0.0)
+            for k in range(i + 2, GROUP):
+                cols[k] = cols[k] - m0 * splat_row(cols[k], i) - m1 * splat_row(cols[k], i + 1)
+            if g + GROUP < STEP:
+                tile = tile - m0 * splat_row(tile, i) - m1 * splat_row(tile, i + 1)
+            inverse = inverse - m0 * splat_row(inverse, i) - m1 * splat_row(inverse, i + 1)
+        done.append(inverse[:GROUP, :])
+        tile, inverse = tile[GROUP:, :], inverse[GROUP:, :]
+    inverse = jnp.concatenate(done, axis=0) * lax.rsqrt(jnp.concatenate(pivots, axis=0))
+    return inverse[:, :STEP]
+
+
+def small_inverse(tile, off):
+    row = lax.broadcasted_iota(jnp.int32, tile.shape, 0)
+    lane = lax.broadcasted_iota(jnp.int32, tile.shape, 1)
+    inverse = jnp.where(row == lane, 1.0, 0.0).astype(F32)
     for g in range(0, STEP, GROUP):
         cols = [jnp.broadcast_to(tile[:, off + g + i : off + g + i + 1], tile.shape) for i in range(GROUP)]
         for i in range(GROUP):
             j = g + i
-            pivot = splat_row(cols[i], j)
-            scale = 1.0 / pivot
-            if chol:
-                m = jnp.where(row > j, cols[i] * scale, 0.0)
-                pivots = jnp.where(row == j, pivot, pivots)
-            else:
-                m = jnp.where(row == j, 1.0 - scale, cols[i] * scale)
+            scale = 1.0 / splat_row(cols[i], j)
+            m = jnp.where(row == j, 1.0 - scale, cols[i] * scale)
             for k in range(i + 1, GROUP):
                 cols[k] = cols[k] - m * splat_row(cols[k], j)
             tile = tile - m * splat_row(tile, j)
             inverse = inverse - m * splat_row(inverse, j)
-    if chol:
-        inverse = inverse * lax.rsqrt(pivots)
     return inverse[:, :STEP]
+
+
+def cholesky_inverse(gram, work, out, halfway=None):
+    size = gram.shape[0]
+    diagonal = jnp.where(identity(size) > 0.0, gram, 0.0)
+    across = lax.rsqrt(jnp.sum(diagonal, axis=0, keepdims=True))
+    work[...] = gram * across * lax.rsqrt(jnp.sum(diagonal, axis=1, keepdims=True))
+    eliminate(work, out, True, halfway)
+    out[...] = out[...] * across
 
 
 def eliminate(work, out, chol, halfway=None):
@@ -176,7 +204,8 @@
         if halfway is not None and 2 * at == size:
             halfway()
         base = at // 128 * 128
-        inverse = small_inverse(work[at:end, base : base + 128], at - base, chol)
+        tile = work[at:end, base : base + 128]
+        inverse = small_factor(tile, at - base) if chol else small_inverse(tile, at - base)
         strip = jnp.where(
             (lane >= at) & (lane < end), jnp.where(lane - at == row, 1.0, 0.0), work[at:end, :]
         )
@@ -210,8 +239,8 @@
 
 def main_kernel(
     rows, cols, a_hbm, z_hbm,
-    y_out, yt_out, v_out, vt_out, c_out, t_out, k_out,
-    alin, zlin, a, z, panel, panel_t, gram, landed, g_out, top_out, rows_out, cols_out, work, w,
+    y_out, yt_out, x_out, xt_out, tk_out,
+    v_out, vt_out, c_out, t_out, k_out, alin, zlin, a, z, panel, panel_t, gram, landed, g_out, top_out, rows_out, cols_out, work, w,
     v, v_half, v_sum, v_land, vt, vt_land, c, c_half, c_sum, c_land, c_row, t, t_land,
     *sems,
 ):
@@ -246,24 +275,34 @@
     def cut(axis, size, me, root, src, dst):
         return Scatter(axis, size, me, root, next(sems), next(sems), src, dst)
 
-    def ring(ref):
-        return Chips(cols, q, next(sems), next(sems), next(sems), next(sems), ref)
+    def ring(at):
+        return Chips(cols, q, next(sems), next(sems), next(sems), next(sems), at)
+
+    tall, flat = slab // 2, piece // 2
+    halves = [(pl.ds(0, tall), pl.ds(0, flat)), (pl.ds(tall, tall), pl.ds(flat, flat))]
 
     reduce = fan("row", rows, p, lambda to: gram.at[to], lambda at: landed.at[at])
     g_wide = fan("row", rows, p, lambda to: g_out.at[p], lambda at: g_out.at[at])
     t_wide = fan("row", rows, p, lambda to: top_out.at[p], lambda at: top_out.at[at])
     c_wide = fan("row", rows, p, lambda to: cols_out.at[p], lambda at: cols_out.at[at])
-    vt_cut = fan("row", rows, p, lambda to: vt.at[to], lambda at: vt_land.at[at])
+    vt_cut = [
+        fan("row", rows, p, lambda to, part=part: vt.at[to, part], lambda at, part=part: vt_land.at[at, part])
+        for _, part in halves
+    ]
     pt_cut = fan("row", rows, p, lambda to: t.at[to], lambda at: t_land.at[at])
     pc_wide = fan("row", rows, p, lambda to: c_row.at[p], lambda at: c_row.at[at])
-    vt_all = fan("row", rows, p, lambda to: vt_out.at[p], lambda at: vt_out.at[at])
+    vt_all = [
+        fan("row", rows, p, lambda to, part=part: vt_out.at[p, part], lambda at, part=part: vt_out.at[at, part])
+        for _, part in halves
+    ]
     pt_all = fan("row", rows, p, lambda to: t_out.at[p], lambda at: t_out.at[at])
     g_down = cut("col", cols, q, 0, lambda to: g_out.at[p], lambda to: g_out.at[p])
     t_cut = cut("row", rows, p, 1, top_piece, lambda to: top_out.at[to])
     t_down = cut("col", cols, q, 0, lambda to: top_out.at[p], lambda to: top_out.at[p])
     r_cut = cut("col", cols, q, 0, row_piece, lambda to: rows_out.at[to])
     c_cut = cut("row", rows, p, 0, lambda to: panel_t.at[to], lambda to: cols_out.at[to])
-    r_wide, v_all, c_all = ring(rows_out), ring(v_out), ring(c_out)
+    r_wide, c_all = ring(lambda i: rows_out.at[i]), ring(lambda i: c_out.at[i])
+    v_all = [ring(lambda i, part=part: v_out.at[i, part]) for part, _ in halves]
 
     met()
 
@@ -340,19 +379,18 @@
         z[:, 128 * at : 128 * (at + 1)] = strip_of(zlin, 0, z.shape[0], at)
     g_wide.wait_recv()
 
-    work[...] = g_out[...].reshape(band, band)
-    eliminate(work, w, True, r_wide.relay)
-
-    def along(src, land):
+    cholesky_inverse(g_out[...].reshape(band, band), work, w, r_wide.relay)
+
+    def along(src, land, part):
         ss, rs = next(sems), next(sems)
 
         def copy(k):
             to = lax.rem(my_z + 1 + k, chips)
-            return send(src.at[to], land.at[my_z], ss.at[k], rs.at[my_z], "col", 2 * to + core)
+            return send(src.at[to, part], land.at[my_z, part], ss.at[k], rs.at[my_z], "col", 2 * to + core)
 
         def recv(k):
             at = lax.rem(my_z + 1 + k, chips)
-            send(src.at[at], land.at[at], ss.at[k], rs.at[at], "col", 2 * at + core).wait_recv()
+            send(src.at[at, part], land.at[at, part], ss.at[k], rs.at[at], "col", 2 * at + core).wait_recv()
 
         return copy, recv
 
@@ -376,15 +414,17 @@
         y_out[:band, :] = y_out[:band, :] + identity(band)
 
     vt[...] = dot(y_out[...], a[...], 0, 0).reshape(vt.shape)
-    vt_cut.start()
+    vt_cut[0].start()
+    vt_cut[1].start()
     v_swap.wait_recv()
 
     def v_add(i):
         v_sum[i] = v[core, i] + v_half[i]
 
     loop(chips, v_add)
-    v_copy, v_recv = along(v_sum, v_land)
-    loop(chips - 1, lambda k: v_copy(k).start())
+    v_along = [along(v_sum, v_land, part) for part, _ in halves]
+    for copy, _ in v_along:
+        loop(chips - 1, lambda k, copy=copy: copy(k).start())
     inner = dot(y_out[...], image, 0, 0)
     for i in range(cols):
         c[i % 2, i // 2] = inner[i * piece : (i + 1) * piece, :]
@@ -395,7 +435,7 @@
     vt_land[p] = vt[p]
     t_land[p] = t[p]
 
-    c_copy, c_recv = along(c_sum, c_land)
+    c_copy, c_recv = along(c_sum, c_land, pl.ds(0, piece))
     c_swap.wait_recv()
 
     def c_add(i):
@@ -408,34 +448,41 @@
 
     t_wide.wait_recv()
     k_out[...] = identity(band) + dot(top_out[...].reshape(band, band), w[...], 1, 1, HIGHEST)
-    eliminate(k_out, None, False)
-
+    def send_on(n):
+        tall_part, flat_part = halves[n]
+        loop(chips - 1, v_along[n][1])
+        v_out[q, tall_part] = total(v_land.at[:, tall_part])
+        v_all[n].start()
+        vt_cut[n].wait_recv()
+        vt_out[p, flat_part] = total(vt_land.at[:, flat_part])
+        vt_all[n].start()
+
+    eliminate(k_out, None, False, lambda: send_on(0))
     loop(chips - 1, c_recv)
     c_row[p] = total(c_land)
     pc_wide.start()
-
-    vt_cut.wait_recv()
-    vt_out[p] = total(vt_land)
-    vt_all.start()
-
-    loop(chips - 1, v_recv)
-    v_out[q] = total(v_land)
-    v_all.start()
-
+    send_on(1)
     pt_cut.wait_recv()
     t_out[p] = total(t_land)
     pt_all.start()
-
+    v_all[0].relay()
     pc_wide.wait_recv()
     c_out[q] = total(c_row)
     c_all.start()
-
-    v_all.relay()
+    v_all[1].relay()
     c_all.relay()
-    vt_all.wait_recv()
+
+    vt_all[0].wait_recv()
+    vt_all[1].wait_recv()
+    c_all.finish()
+    inner_half = 0.5 * dot(dot(k_out[...], c_out[...].reshape(band, band), 0, 0), k_out[...], 1, 0)
+    xt_out[...] = dot(k_out[...], vt_out[...].reshape(band, height), 0, 0) - dot(inner_half, yt_out[...], 0, 0)
+    x_out[...] = dot(y_out[...], inner_half, 1, 0)
     pt_all.wait_recv()
-    v_all.finish()
-    c_all.finish()
+    tk_out[...] = dot(t_out[...].reshape(tk_out.shape), k_out[...], 1, 0)
+    v_all[0].finish()
+    v_all[1].finish()
+    x_out[...] = dot(v_out[...].reshape(height, band), k_out[...], 1, 0) - x_out[...]
 
     @pl.when(first)
     def _():
@@ -455,9 +502,10 @@
 
     v_swap.wait_send()
     c_swap.wait_send()
-    loop(chips - 1, lambda k: v_copy(k).wait_send())
+    for copy, _ in v_along:
+        loop(chips - 1, lambda k, copy=copy: copy(k).wait_send())
     loop(chips - 1, lambda k: c_copy(k).wait_send())
-    for done in (g_wide, t_wide, c_wide, vt_cut, pt_cut, pc_wide, vt_all, pt_all):
+    for done in (g_wide, t_wide, c_wide, *vt_cut, pt_cut, pc_wide, *vt_all, pt_all):
         done.wait_send()
 
 
@@ -473,9 +521,9 @@
     vmem = pl.BlockSpec(memory_space=pltpu.VMEM)
     flat = (height, band)
     small = (rows, piece, band)
-    outs = [flat, (band, height), (cols, slab, band), (rows, piece, height), (cols, piece, band), (rows, tp, band), (band, band)]
+    outs = [flat, (band, height), flat, (band, height), (count, band)]
     scratch = [
-        alin.shape, zlin.shape, (height, height), (count, height), flat, (rows, piece, height), small, small, small, small,
+        (cols, slab, band), (rows, piece, height), (cols, piece, band), (rows, tp, band), (band, band), alin.shape, zlin.shape, (height, height), (count, height), flat, (rows, piece, height), small, small, small, small,
         (cols, slab, band), (rows, piece, height), (band, band), (band, band),
         (2, chips, slab, band), (chips, slab, band), (chips, slab, band), (chips, slab, band),
         (rows, piece, height), (rows, piece, height),
@@ -487,37 +535,52 @@
         out_shape=tuple(jax.ShapeDtypeStruct(s, F32) for s in outs),
         in_specs=[pl.BlockSpec(memory_space=pltpu.HBM)] * 2,
         out_specs=(vmem,) * len(outs),
-        scratch_shapes=[pltpu.VMEM(s, F32) for s in scratch] + [dma] * 2 + fan * 9 + cut * 5 + ring * 3 + [dma] * 2 + half + [dma] * 2 + half,
+        scratch_shapes=[pltpu.VMEM(s, F32) for s in scratch] + [dma] * 2 + fan * 11 + cut * 5 + ring * 4 + [dma] * 2 + half * 2 + [dma] * 2 + half,
         compiler_params=pltpu.CompilerParams(collective_id=0, has_side_effects=True, vmem_limit_bytes=50 * 2**20),
         name="main",
     )(alin, zlin)
 
 
-def update_kernel(alin, zlin, y, yt, v, vt, c, t, k, a_out, z_out):
+def update_kernel(alin, zlin, y, yt, x, xt, tk, a_hbm, z_hbm, a_out, z_out, sems):
     height, band = y.shape
     count = zlin.shape[0] // WIDE
-    image, image_t = v[...].reshape(height, band), vt[...].reshape(band, height)
-    half = 0.5 * dot(dot(k[...], c[...].reshape(band, band), 0, 0), k[...], 1, 0)
-    x = dot(image, k[...], 1, 0) - dot(y[...], half, 1, 0)
-    xt = dot(k[...], image_t, 0, 0) - dot(half, yt[...], 0, 0)
-    tk = dot(t[...].reshape(count, band), k[...], 1, 0)
-    for lo in range(0, height, band):
-        move = dot(x, yt[:, lo : lo + band], 1, 0) + dot(y[...], xt[:, lo : lo + band], 1, 0)
-        turn = dot(tk, y[lo : lo + band, :], 1, 1)
-        for i in range(band // 128):
-            at = lo // 128 + i
-            lanes = slice(128 * i, 128 * (i + 1))
-            a_out[pl.ds(at, height, stride=WIDE), :] = strip_of(alin, 0, height, at) - move[:, lanes]
-            z_out[pl.ds(at, count, stride=WIDE), :] = strip_of(zlin, 0, count, at) - turn[:, lanes]
+    copies = []
+
+    def put(src, dst, lines, n):
+        copies.append(pltpu.make_async_copy(src.at[lines, :], dst.at[lines, :], sems.at[n]))
+        copies[-1].start()
+
+    parts = height // band
+    for n in range(parts):
+        lo = n * band
+        block = slice(lo, lo + band)
+        move = dot(x[block, :], yt[...], 1, 0) + dot(y[block, :], xt[...], 1, 0)
+        for at in range(WIDE):
+            lines = pl.ds(lo * WIDE + at, band, stride=WIDE)
+            a_out[lines, :] = alin[lines, :] - move[:, 128 * at : 128 * (at + 1)]
+        put(a_out, a_hbm, pl.ds(lo * WIDE, band * WIDE), n)
+    turn = dot(tk[...], y[...], 1, 1)
+    for at in range(WIDE):
+        lines = pl.ds(at, count, stride=WIDE)
+        z_out[lines, :] = zlin[lines, :] - turn[:, 128 * at : 128 * (at + 1)]
+    put(z_out, z_hbm, pl.ds(0, count * WIDE), parts)
+    for copy in copies:
+        copy.wait()
 
 
 def update(alin, zlin, *rest):
     vmem = pl.BlockSpec(memory_space=pltpu.VMEM)
+    height, band = rest[0].shape
     return pl.pallas_call(
         update_kernel,
         out_shape=(jax.ShapeDtypeStruct(alin.shape, F32), jax.ShapeDtypeStruct(zlin.shape, F32)),
         in_specs=[vmem] * (2 + len(rest)),
-        out_specs=(vmem,) * 2,
+        out_specs=(pl.BlockSpec(memory_space=pltpu.HBM),) * 2,
+        scratch_shapes=[
+            pltpu.VMEM(alin.shape, F32),
+            pltpu.VMEM(zlin.shape, F32),
+            pltpu.SemaphoreType.DMA((height // band + 1,)),
+        ],
         compiler_params=pltpu.CompilerParams(vmem_limit_bytes=24 * 2**20),
         name="update",
     )(alin, zlin, *rest)

time: 90.2 us -> 88.7 us (0.983); the launches traced: 90.2 us -> 87.4 us
  Pallas kernels: 89.5 us -> 86.6 us
    pallas_call x1, Pallas kernels: 5.85 us -> 3.69 us  [update(): pl.pallas_call(update_kernel, out_shape=(jax.ShapeDtypeStruct(alin.shape,...]
where the time goes in v3:
time: 88.7 us; the launch traced here: 87.4 us
  Pallas kernels  86.6 us (98%)
    pallas_call x1, Pallas kernels, main(): pl.pallas_call(functools.partial(main_kernel, rows, cols), out_shape=tupl...  82.9 us
    pallas_call x1, Pallas kernels, update(): pl.pallas_call(update_kernel, out_shape=(jax.ShapeDtypeStruct(alin.shape,...  3.69 us

profile of v3, /device:TPU:6, one launch (start us, length us, event | category | flops | bytes accessed | tf_op | source)
XLA Modules:
  0.0 87.4 jit_solution(15759471455596561276)
XLA Ops:
  0.6 0.0 copy-start.1
  0.6 0.0 copy-start
  0.6 82.9 %main.1 = (f32[768,256]{1,0:T(8,128)S(1)}, f32[256,768]{1,0:T(8,128)S(1)}, f32[768,256]{1,0:T(8,128)S(1)}, f32[256,768]{1,0:T(8,128)S(1)}, f32[256,256]{1,0:T(8,128)S(1)}) custom-call(f32[4608,128]{1,0:T(8,128)} %bitcast.4, f32[1536,128]{1,0:T(8,128)} %bitcast.6), custom_call_target="tpu_custom_call" | custom-call | tf_op jit(solution)/shard_map/main/pallas_call | solution.py:533
  83.5 0.0 copy-done.1
  83.5 0.0 copy-done
  83.5 3.7 %update.1 = (f32[4608,128]{1,0:T(8,128)}, f32[1536,128]{1,0:T(8,128)}) custom-call(f32[4608,128]{1,0:T(8,128)S(1)} %bitcast.5, f32[1536,128]{1,0:T(8,128)S(1)} %bitcast.7, f32[768,256]{1,0:T(8,128)S(1)} %get-tuple-element.9.y, f32[256,768]{1,0:T(8,128)S(1)} %get-tuple-element.10.yt, f32[768,256]{1,0:T(8,128)S(1)} %get-tuple-element.11.x, ...), custom_call_target="tpu_custom_call" | custom-call | tf_op jit(solution)/shard_map/update/pallas_call | solution.py:574
Async XLA Ops:
  0.6 82.9 %copy-start.1 = (f32[256,3,1,256]{3,2,1,0:T(1,128)S(1)}, f32[256,3,1,256]{3,2,1,0:T(1,128)}, u32[]{:S(2)}) copy-start(f32[256,3,1,256]{3,2,1,0:T(1,128)} %param.3) | copy-start | bytes 2359300
  0.6 82.9 %copy-start = (f32[3,1,256,3,1,256]{5,4,3,2,1,0:T(1,128)S(1)}, f32[3,1,256,3,1,256]{5,4,3,2,1,0:T(1,128)}, u32[]{:S(2)}) copy-start(f32[3,1,256,3,1,256]{5,4,3,2,1,0:T(1,128)} %param.2) | copy-start | bytes 7077892

commit v4 on v3

--- a/solution.py
+++ b/solution.py
@@ -12,6 +12,7 @@
 HIGH = lax.Precision.HIGH
 HIGHEST = lax.Precision.HIGHEST
 STEP = 64
+FINE = 32
 GROUP = 16
 WIDE = 6
 
@@ -173,7 +174,7 @@
     row = lax.broadcasted_iota(jnp.int32, tile.shape, 0)
     lane = lax.broadcasted_iota(jnp.int32, tile.shape, 1)
     inverse = jnp.where(row == lane, 1.0, 0.0).astype(F32)
-    for g in range(0, STEP, GROUP):
+    for g in range(0, FINE, GROUP):
         cols = [jnp.broadcast_to(tile[:, off + g + i : off + g + i + 1], tile.shape) for i in range(GROUP)]
         for i in range(GROUP):
             j = g + i
@@ -183,26 +184,28 @@
                 cols[k] = cols[k] - m * splat_row(cols[k], j)
             tile = tile - m * splat_row(tile, j)
             inverse = inverse - m * splat_row(inverse, j)
-    return inverse[:, :STEP]
-
-
-def cholesky_inverse(gram, work, out, halfway=None):
+    return inverse[:, :FINE]
+
+
+def cholesky_inverse(gram, work, out):
     size = gram.shape[0]
     diagonal = jnp.where(identity(size) > 0.0, gram, 0.0)
     across = lax.rsqrt(jnp.sum(diagonal, axis=0, keepdims=True))
     work[...] = gram * across * lax.rsqrt(jnp.sum(diagonal, axis=1, keepdims=True))
-    eliminate(work, out, True, halfway)
+    eliminate(work, out, True)
     out[...] = out[...] * across
 
 
-def eliminate(work, out, chol, halfway=None):
+def eliminate(work, out, chol, between=()):
     size = work.shape[0]
-    lane = lax.broadcasted_iota(jnp.int32, (STEP, size), 1)
-    row = lax.broadcasted_iota(jnp.int32, (STEP, size), 0)
-    for at in range(0, size, STEP):
-        end = at + STEP
-        if halfway is not None and 2 * at == size:
-            halfway()
+    step = STEP if chol else FINE
+    lane = lax.broadcasted_iota(jnp.int32, (step, size), 1)
+    row = lax.broadcasted_iota(jnp.int32, (step, size), 0)
+    for at in range(0, size, step):
+        end = at + step
+        for when, act in between:
+            if when == at // step:
+                act()
         base = at // 128 * 128
         tile = work[at:end, base : base + 128]
         inverse = small_factor(tile, at - base) if chol else small_inverse(tile, at - base)
@@ -379,7 +382,8 @@
         z[:, 128 * at : 128 * (at + 1)] = strip_of(zlin, 0, z.shape[0], at)
     g_wide.wait_recv()
 
-    cholesky_inverse(g_out[...].reshape(band, band), work, w, r_wide.relay)
+    cholesky_inverse(g_out[...].reshape(band, band), work, w)
+    r_wide.relay()
 
     def along(src, land, part):
         ss, rs = next(sems), next(sems)
@@ -405,6 +409,9 @@
     for i in range(cols):
         v[i % 2, i // 2] = image[i * slab : (i + 1) * slab, :]
     v_swap = send(v.at[1 - core], v_half, next(sems), next(sems), "col", other)
+    v_along = [along(v_sum, v_land, part) for part, _ in halves]
+    c_swap = send(c.at[1 - core], c_half, next(sems), next(sems), "col", other)
+    c_copy, c_recv = along(c_sum, c_land, pl.ds(0, piece))
     v_swap.start()
     r_wide.finish()
     y_out[...] = dot(rows_out[...].reshape(height, band), w[...], 1, 1)
@@ -413,64 +420,68 @@
     def _():
         y_out[:band, :] = y_out[:band, :] + identity(band)
 
-    vt[...] = dot(y_out[...], a[...], 0, 0).reshape(vt.shape)
-    vt_cut[0].start()
-    vt_cut[1].start()
     v_swap.wait_recv()
 
     def v_add(i):
         v_sum[i] = v[core, i] + v_half[i]
 
     loop(chips, v_add)
-    v_along = [along(v_sum, v_land, part) for part, _ in halves]
-    for copy, _ in v_along:
-        loop(chips - 1, lambda k, copy=copy: copy(k).start())
+    loop(chips - 1, lambda k: v_along[0][0](k).start())
     inner = dot(y_out[...], image, 0, 0)
     for i in range(cols):
         c[i % 2, i // 2] = inner[i * piece : (i + 1) * piece, :]
-    c_swap = send(c.at[1 - core], c_half, next(sems), next(sems), "col", other)
     c_swap.start()
+    vt[...] = dot(y_out[...], a[...], 0, 0).reshape(vt.shape)
+    vt_cut[0].start()
+    c_swap.wait_recv()
+
+    def c_add(i):
+        c_sum[i] = c[core, i] + c_half[i]
+
+    loop(chips, c_add)
+    loop(chips - 1, lambda k: c_copy(k).start())
+    loop(chips - 1, lambda k: v_along[1][0](k).start())
+    vt_cut[1].start()
     t[...] = dot(z[...], y_out[...], 1, 0).reshape(t.shape)
-    pt_cut.start()
     vt_land[p] = vt[p]
     t_land[p] = t[p]
-
-    c_copy, c_recv = along(c_sum, c_land, pl.ds(0, piece))
-    c_swap.wait_recv()
-
-    def c_add(i):
-        c_sum[i] = c[core, i] + c_half[i]
-
-    loop(chips, c_add)
-    loop(chips - 1, lambda k: c_copy(k).start())
     v_land[my_z] = v_sum[my_z]
     c_land[my_z] = c_sum[my_z]
 
+    def send_v(n):
+        loop(chips - 1, v_along[n][1])
+        v_out[q, halves[n][0]] = total(v_land.at[:, halves[n][0]])
+        v_all[n].start()
+
+    def send_vt(n):
+        vt_cut[n].wait_recv()
+        vt_out[p, halves[n][1]] = total(vt_land.at[:, halves[n][1]])
+        vt_all[n].start()
+
+    def send_c():
+        loop(chips - 1, c_recv)
+        c_row[p] = total(c_land)
+        pc_wide.start()
+        pt_cut.start()
+
+    def share_c():
+        pc_wide.wait_recv()
+        c_out[q] = total(c_row)
+        c_all.start()
+
     t_wide.wait_recv()
     k_out[...] = identity(band) + dot(top_out[...].reshape(band, band), w[...], 1, 1, HIGHEST)
-    def send_on(n):
-        tall_part, flat_part = halves[n]
-        loop(chips - 1, v_along[n][1])
-        v_out[q, tall_part] = total(v_land.at[:, tall_part])
-        v_all[n].start()
-        vt_cut[n].wait_recv()
-        vt_out[p, flat_part] = total(vt_land.at[:, flat_part])
-        vt_all[n].start()
-
-    eliminate(k_out, None, False, lambda: send_on(0))
-    loop(chips - 1, c_recv)
-    c_row[p] = total(c_land)
-    pc_wide.start()
-    send_on(1)
+    eliminate(
+        k_out, None, False, [(3, send_c), (5, lambda: send_v(0)), (6, lambda: send_vt(0)), (7, share_c)]
+    )
+    send_v(1)
+    send_vt(1)
     pt_cut.wait_recv()
     t_out[p] = total(t_land)
     pt_all.start()
     v_all[0].relay()
-    pc_wide.wait_recv()
-    c_out[q] = total(c_row)
-    c_all.start()
+    c_all.relay()
     v_all[1].relay()
-    c_all.relay()
 
     vt_all[0].wait_recv()
     vt_all[1].wait_recv()

time: 88.7 us -> 89.9 us (1.014); the launches traced: 87.4 us -> 89.9 us
  Pallas kernels: 86.6 us -> 89 us
    pallas_call x1, Pallas kernels: 82.9 us -> 85.3 us  [main(): pl.pallas_call(functools.partial(main_kernel, rows, cols), out_shape=tupl...]
where the time goes in v4:
time: 89.9 us
  Pallas kernels  89 us (99%)
    pallas_call x1, Pallas kernels, main(): pl.pallas_call(functools.partial(main_kernel, rows, cols), out_shape=tupl...  85.3 us
    pallas_call x1, Pallas kernels, update(): pl.pallas_call(update_kernel, out_shape=(jax.ShapeDtypeStruct(alin.shape,...  3.69 us

profile of v4, /device:TPU:6, one launch (start us, length us, event | category | flops | bytes accessed | tf_op | source)
XLA Modules:
  0.0 89.9 jit_solution(1072408378672608626)
XLA Ops:
  0.6 0.0 copy-start.1
  0.6 0.0 copy-start
  0.6 85.3 %main.1 = (f32[768,256]{1,0:T(8,128)S(1)}, f32[256,768]{1,0:T(8,128)S(1)}, f32[768,256]{1,0:T(8,128)S(1)}, f32[256,768]{1,0:T(8,128)S(1)}, f32[256,256]{1,0:T(8,128)S(1)}) custom-call(f32[4608,128]{1,0:T(8,128)} %bitcast.4, f32[1536,128]{1,0:T(8,128)} %bitcast.6), custom_call_target="tpu_custom_call" | custom-call | tf_op jit(solution)/shard_map/main/pallas_call | solution.py:544
  86.0 0.0 copy-done.1
  86.0 0.0 copy-done
  86.0 3.7 %update.1 = (f32[4608,128]{1,0:T(8,128)}, f32[1536,128]{1,0:T(8,128)}) custom-call(f32[4608,128]{1,0:T(8,128)S(1)} %bitcast.5, f32[1536,128]{1,0:T(8,128)S(1)} %bitcast.7, f32[768,256]{1,0:T(8,128)S(1)} %get-tuple-element.9.y, f32[256,768]{1,0:T(8,128)S(1)} %get-tuple-element.10.yt, f32[768,256]{1,0:T(8,128)S(1)} %get-tuple-element.11.x, ...), custom_call_target="tpu_custom_call" | custom-call | tf_op jit(solution)/shard_map/update/pallas_call | solution.py:585
Async XLA Ops:
  0.6 85.3 %copy-start.1 = (f32[256,3,1,256]{3,2,1,0:T(1,128)S(1)}, f32[256,3,1,256]{3,2,1,0:T(1,128)}, u32[]{:S(2)}) copy-start(f32[256,3,1,256]{3,2,1,0:T(1,128)} %param.3) | copy-start | bytes 2359300
  0.6 85.3 %copy-start = (f32[3,1,256,3,1,256]{5,4,3,2,1,0:T(1,128)S(1)}, f32[3,1,256,3,1,256]{5,4,3,2,1,0:T(1,128)}, u32[]{:S(2)}) copy-start(f32[3,1,256,3,1,256]{5,4,3,2,1,0:T(1,128)} %param.2) | copy-start | bytes 7077892

commit v5 on v4

--- a/solution.py
+++ b/solution.py
@@ -187,12 +187,12 @@
     return inverse[:, :FINE]
 
 
-def cholesky_inverse(gram, work, out):
+def cholesky_inverse(gram, work, out, between=()):
     size = gram.shape[0]
     diagonal = jnp.where(identity(size) > 0.0, gram, 0.0)
     across = lax.rsqrt(jnp.sum(diagonal, axis=0, keepdims=True))
     work[...] = gram * across * lax.rsqrt(jnp.sum(diagonal, axis=1, keepdims=True))
-    eliminate(work, out, True)
+    eliminate(work, out, True, between)
     out[...] = out[...] * across
 
 
@@ -341,49 +341,50 @@
         g_out[p] = total(landed)
         g_down.start()
 
-    @pl.when(p == 0)
-    def _():
-        cols_out[0] = panel_t[0]
-
-    @pl.when(jnp.logical_not(first))
-    def _():
-        g_down.wait_recv()
-
-    g_wide.start()
-
-    @pl.when(jnp.logical_not(first))
-    def _():
-        r_cut.wait_recv()
-
-    r_wide.start()
-
-    @pl.when(p != 0)
-    def _():
-        c_cut.wait_recv()
-
-    c_wide.start()
-
-    @pl.when(first)
-    def _():
         @pl.when(p != 1)
         def _():
             t_cut.wait_recv()
 
         t_down.start()
 
+    @pl.when(p == 0)
+    def _():
+        cols_out[0] = panel_t[0]
+
     @pl.when(jnp.logical_not(first))
     def _():
-        t_down.wait_recv()
-
-    t_wide.start()
+        g_down.wait_recv()
+
+    g_wide.start()
+
+    @pl.when(jnp.logical_not(first))
+    def _():
+        r_cut.wait_recv()
+
+    r_wide.start()
+
+    @pl.when(p != 0)
+    def _():
+        c_cut.wait_recv()
+
+    c_wide.start()
+
     z_in.wait()
     for at in range(WIDE):
         a[:, 128 * at : 128 * (at + 1)] = strip_of(alin, 0, height, at)
         z[:, 128 * at : 128 * (at + 1)] = strip_of(zlin, 0, z.shape[0], at)
     g_wide.wait_recv()
 
-    cholesky_inverse(g_out[...].reshape(band, band), work, w)
-    r_wide.relay()
+    def meanwhile():
+        r_wide.relay()
+
+        @pl.when(jnp.logical_not(first))
+        def _():
+            t_down.wait_recv()
+
+        t_wide.start()
+
+    cholesky_inverse(g_out[...].reshape(band, band), work, w, [(band // STEP // 2, meanwhile)])
 
     def along(src, land, part):
         ss, rs = next(sems), next(sems)
@@ -443,6 +444,7 @@
     loop(chips - 1, lambda k: v_along[1][0](k).start())
     vt_cut[1].start()
     t[...] = dot(z[...], y_out[...], 1, 0).reshape(t.shape)
+    pt_cut.start()
     vt_land[p] = vt[p]
     t_land[p] = t[p]
     v_land[my_z] = v_sum[my_z]
@@ -462,7 +464,6 @@
         loop(chips - 1, c_recv)
         c_row[p] = total(c_land)
         pc_wide.start()
-        pt_cut.start()
 
     def share_c():
         pc_wide.wait_recv()
@@ -472,16 +473,17 @@
     t_wide.wait_recv()
     k_out[...] = identity(band) + dot(top_out[...].reshape(band, band), w[...], 1, 1, HIGHEST)
     eliminate(
-        k_out, None, False, [(3, send_c), (5, lambda: send_v(0)), (6, lambda: send_vt(0)), (7, share_c)]
+        k_out, None, False, [(4, send_c), (5, lambda: send_v(0)), (7, lambda: send_vt(0))]
     )
     send_v(1)
+    share_c()
     send_vt(1)
     pt_cut.wait_recv()
     t_out[p] = total(t_land)
     pt_all.start()
     v_all[0].relay()
+    v_all[1].relay()
     c_all.relay()
-    v_all[1].relay()
 
     vt_all[0].wait_recv()
     vt_all[1].wait_recv()

time: 89.9 us -> 88.5 us (0.984)
  Pallas kernels: 89 us -> 87.5 us
    pallas_call x1, Pallas kernels: 85.3 us -> 83.8 us  [main(): pl.pallas_call(functools.partial(main_kernel, rows, cols), out_shape=tupl...]
where the time goes in v5:
time: 88.5 us; the launch traced here: 88.4 us
  Pallas kernels  87.5 us (99%)
    pallas_call x1, Pallas kernels, main(): pl.pallas_call(functools.partial(main_kernel, rows, cols), out_shape=tupl...  83.8 us
    pallas_call x1, Pallas kernels, update(): pl.pallas_call(update_kernel, out_shape=(jax.ShapeDtypeStruct(alin.shape,...  3.69 us

profile of v5, /device:TPU:6, one launch (start us, length us, event | category | flops | bytes accessed | tf_op | source)
XLA Modules:
  0.0 88.4 jit_solution(4579099787127280187)
XLA Ops:
  0.6 0.0 copy-start.1
  0.6 0.0 copy-start
  0.6 83.8 %main.1 = (f32[768,256]{1,0:T(8,128)S(1)}, f32[256,768]{1,0:T(8,128)S(1)}, f32[768,256]{1,0:T(8,128)S(1)}, f32[256,768]{1,0:T(8,128)S(1)}, f32[256,256]{1,0:T(8,128)S(1)}) custom-call(f32[4608,128]{1,0:T(8,128)} %bitcast.4, f32[1536,128]{1,0:T(8,128)} %bitcast.6), custom_call_target="tpu_custom_call" | custom-call | tf_op jit(solution)/shard_map/main/pallas_call | solution.py:546
  84.5 0.0 copy-done.1
  84.5 0.0 copy-done
  84.5 3.7 %update.1 = (f32[4608,128]{1,0:T(8,128)}, f32[1536,128]{1,0:T(8,128)}) custom-call(f32[4608,128]{1,0:T(8,128)S(1)} %bitcast.5, f32[1536,128]{1,0:T(8,128)S(1)} %bitcast.7, f32[768,256]{1,0:T(8,128)S(1)} %get-tuple-element.9.y, f32[256,768]{1,0:T(8,128)S(1)} %get-tuple-element.10.yt, f32[768,256]{1,0:T(8,128)S(1)} %get-tuple-element.11.x, ...), custom_call_target="tpu_custom_call" | custom-call | tf_op jit(solution)/shard_map/update/pallas_call | solution.py:587
Async XLA Ops:
  0.6 83.9 %copy-start.1 = (f32[256,3,1,256]{3,2,1,0:T(1,128)S(1)}, f32[256,3,1,256]{3,2,1,0:T(1,128)}, u32[]{:S(2)}) copy-start(f32[256,3,1,256]{3,2,1,0:T(1,128)} %param.3) | copy-start | bytes 2359300
  0.6 83.9 %copy-start = (f32[3,1,256,3,1,256]{5,4,3,2,1,0:T(1,128)S(1)}, f32[3,1,256,3,1,256]{5,4,3,2,1,0:T(1,128)}, u32[]{:S(2)}) copy-start(f32[3,1,256,3,1,256]{5,4,3,2,1,0:T(1,128)} %param.2) | copy-start | bytes 7077892
